TPU v7x, 256 devices: a whole 4x4x8 slice. The times are simulated.
256 devices in a mesh: time: 64 (over z_lo, y, x, core), chan: 4 (over z_hi).
Axes of the slice: x: 4, y: 4, z: 8 (z_hi: 4, z_lo: 2; z = z_hi * 2 + z_lo), core: 2. Of those that a mesh axis runs over, the one named last changes fastest.
Arguments:
- decay_rate: float32 [4, 32768, 2560], P(None, 'time', 'chan'), may hold values from 0.2 to 2
- drive_in: bfloat16 [4, 32768, 2560], P(None, 'time', 'chan'), may hold values from -6 to 6
- gate_in: bfloat16 [4, 32768, 2560], P(None, 'time', 'chan'), may hold values from -6 to 6
- norm_gain: float32 [2560], P('chan'), may hold values from 0.25 to 1.75
Outputs:
- filtered: bfloat16 [4, 32768, 2560], P(None, 'time', 'chan')
All inputs are finite; a program needn't handle non-finite values.
Results may differ from a plain program's by a relative error of at most 0.0015.
Values sent between devices are 32-bit elements.
No kernel may reach another device: no remote copies, remote signals or barrier semaphores. Data moves between devices by JAX's collectives and lax.ppermute only.
A program may use at most 128 MiB of HBM per device.

v0:
```python
import jax
import jax.numpy as jnp
from jax import lax
from jax.sharding import Mesh
from jax.sharding import PartitionSpec as P

TIME = ("time_0", "time_1", "time_2", "time_3")


def nothing_yet(x, identity):
    return jax.tree.map(
        lambda part, zero: jnp.zeros_like(part) + jnp.asarray(zero, part.dtype), x, identity
    )


def entering(x, axes, combine, identity, reverse):
    before = start = nothing_yet(x, identity)
    so_far = x
    for axis in reversed(axes):
        peers, here = lax.axis_size(axis), lax.axis_index(axis)
        pieces = jax.tree.map(lambda part: lax.all_gather(part, axis), so_far)
        inside, so_far = start, start
        for k in reversed(range(peers)) if reverse else range(peers):
            passed = k > here if reverse else k < here
            so_far = combine(so_far, jax.tree.map(lambda part: part[k], pieces))
            inside = jax.tree.map(lambda new, old: jnp.where(passed, new, old), so_far, inside)
        before = combine(inside, before)
    return before


def gathered_total(x, axis):
    return lax.all_gather(x, axis).sum(0)


def join_pair(earlier, later):
    return (earlier[0] * later[0], later[0] * earlier[1] + later[1])


def body(decay_rate, drive_in, gate_in, norm_gain):
    total_length = decay_rate.shape[1] * lax.axis_size(TIME)
    keep = jnp.exp(-decay_rate / total_length)
    push = drive_in.astype(jnp.float32) * total_length ** (-0.5)
    steps = -decay_rate / total_length
    logs = jnp.sum(steps, axis=1, keepdims=True) - jnp.cumsum(steps, axis=1)
    summary = (jnp.exp(jnp.sum(steps, axis=1)), jnp.sum(jnp.exp(logs) * push, axis=1))
    entering_forward = entering(
        summary, TIME, join_pair, (jnp.ones_like(keep[:, 0]), jnp.zeros_like(push[:, 0])), False
    )
    started = push.at[:, 0].add(keep[:, 0] * entering_forward[1])
    forward = lax.associative_scan(join_pair, (keep, started), axis=1)[1]
    gated = forward * jax.nn.sigmoid(gate_in.astype(jnp.float32))
    power = gathered_total(jnp.sum(gated * gated, axis=-1, keepdims=True), "chan") / (
        gated.shape[-1] * lax.axis_size("chan")
    )
    filtered = (gated * lax.rsqrt(power + 1e-06) * norm_gain).astype(jnp.bfloat16)
    return filtered


def solution(mesh):
    split = Mesh(
        mesh.devices.reshape(2, 4, 4, 2, mesh.shape["chan"]),
        ("time_0", "time_1", "time_2", "time_3", "chan"),
    )
    in_specs = (P(None, TIME, "chan"), P(None, TIME, "chan"), P(None, TIME, "chan"), P("chan"))
    out_specs = P(None, TIME, "chan")
    return jax.shard_map(body, mesh=split, in_specs=in_specs, out_specs=out_specs, check_vma=False)
```

profile of v0, /device:TPU:2, one launch (start us, length us, event | category | flops | bytes accessed | tf_op | source)
XLA Modules:
  0.0 295.3 jit_solution(13377627184251010593)
XLA Ops:
  0.0 7.1 %fusion.24 = (f32[4,640]{1,0:T(4,128)S(1)}, f32[4,512,640]{2,1,0:T(8,128)}, f32[4,512,640]{2,1,0:T(8,128)}) fusion(f32[4,512,640]{2,1,0:T(8,128)} %param.6), kind=kLoop, calls=%fused_computation.120 | loop fusion | flops 3929600 | bytes 15738880 | tf_op jit(solution)/shard_map/reduce_sum | solution.py:45
  7.1 8.2 %fusion.2 = f32[4,640,4,128]{1,2,3,0:T(4,128)} fusion(f32[4,640,4,128]{1,3,2,0:T(8,128)} %bitcast.171), kind=kOutput, calls=%fused_computation.4 | output fusion | flops 166461440 | bytes 10485760 | tf_op jit(solution)/shard_map/reduce-window
  26.3 11.9 %all_gather.43 = f32[4,4,640]{2,1,0:T(4,128)S(1)} all-gather(f32[1,4,640]{2,1,0:T(4,128)S(1)} %copy.27), channel_id=1, replica_groups=mesh['time_0'=2,'time_1'=4,'time_2'=4,'time_3'=2,'chan'=4] {'time_2'}, dimensions={0}, use_global_device_ids=true | all-gather | bytes 51200 | tf_op jit(solution)/shard_map/all_gather | solution.py:21
  38.2 11.8 %all_gather.38 = f32[4,4,640]{2,1,0:T(4,128)S(1)} all-gather(f32[1,4,640]{2,1,0:T(4,128)S(1)} %copy.10), channel_id=1, replica_groups=mesh['time_0'=2,'time_1'=4,'time_2'=4,'time_3'=2,'chan'=4] {'time_2'}, dimensions={0}, use_global_device_ids=true | all-gather | bytes 51200 | tf_op jit(solution)/shard_map/all_gather | solution.py:21
  50.1 12.4 %all_gather.44 = f32[4,4,640]{2,1,0:T(4,128)S(1)} all-gather(f32[1,4,640]{2,1,0:T(4,128)S(1)} %copy.32), channel_id=1, replica_groups=mesh['time_0'=2,'time_1'=4,'time_2'=4,'time_3'=2,'chan'=4] {'time_1'}, dimensions={0}, use_global_device_ids=true | all-gather | bytes 51200 | tf_op jit(solution)/shard_map/all_gather | solution.py:21
  62.5 11.8 %all_gather.39 = f32[4,4,640]{2,1,0:T(4,128)S(1)} all-gather(f32[1,4,640]{2,1,0:T(4,128)S(1)} %copy.15), channel_id=1, replica_groups=mesh['time_0'=2,'time_1'=4,'time_2'=4,'time_3'=2,'chan'=4] {'time_1'}, dimensions={0}, use_global_device_ids=true | all-gather | bytes 51200 | tf_op jit(solution)/shard_map/all_gather | solution.py:21
  74.4 4.4 %all_gather.40 = f32[2,4,640]{2,1,0:T(4,128)S(1)} all-gather(f32[1,4,640]{2,1,0:T(4,128)S(1)} %copy.20), channel_id=1, replica_groups=mesh['time_0'=2,'time_1'=4,'time_2'=4,'time_3'=2,'chan'=4] {'time_0'}, dimensions={0}, use_global_device_ids=true | all-gather | bytes 30720 | tf_op jit(solution)/shard_map/all_gather | solution.py:21
  78.7 4.5 %all_gather.45 = f32[2,4,640]{2,1,0:T(4,128)S(1)} all-gather(f32[1,4,640]{2,1,0:T(4,128)S(1)} %copy.37), channel_id=1, replica_groups=mesh['time_0'=2,'time_1'=4,'time_2'=4,'time_3'=2,'chan'=4] {'time_0'}, dimensions={0}, use_global_device_ids=true | all-gather | bytes 30720 | tf_op jit(solution)/shard_map/all_gather | solution.py:21
  85.9 14.1 %slice.401 = f32[4,255,640]{2,1,0:T(8,128)} slice(f32[4,512,640]{2,1,0:T(8,128)} %scatter-add.4), slice={[0:4:1], [2:512:2], [0:640:1]} | slice | bytes 5222400 | tf_op jit(solution)/shard_map/slice | solution.py:50
  100.0 14.0 %slice.339 = f32[4,256,640]{2,1,0:T(8,128)} slice(f32[4,512,640]{2,1,0:T(8,128)} %scatter-add.4), slice={[0:4:1], [1:512:2], [0:640:1]} | slice | bytes 5242880 | tf_op jit(solution)/shard_map/slice | solution.py:50
  114.0 14.0 %slice.338 = f32[4,256,640]{2,1,0:T(8,128)} slice(f32[4,512,640]{2,1,0:T(8,128)} %scatter-add.4), slice={[0:4:1], [0:511:2], [0:640:1]} | slice | bytes 5242880 | tf_op jit(solution)/shard_map/slice | solution.py:50
  128.0 14.0 %slice.341 = f32[4,256,640]{2,1,0:T(8,128)} slice(f32[4,512,640]{2,1,0:T(8,128)} %get-tuple-element.20), slice={[0:4:1], [0:511:2], [0:640:1]} | slice | bytes 5242880 | tf_op jit(solution)/shard_map/slice | solution.py:50
  142.0 14.0 %slice.337 = f32[4,256,640]{2,1,0:T(8,128)} slice(f32[4,512,640]{2,1,0:T(8,128)} %get-tuple-element.20), slice={[0:4:1], [1:512:2], [0:640:1]} | slice | bytes 5242880 | tf_op jit(solution)/shard_map/slice | solution.py:50
  156.0 6.1 %fusion.26 = (f32[4,256,640]{2,1,0:T(8,128)}, f32[4,256,640]{2,1,0:T(8,128)S(1)}) fusion(f32[4,256,640]{2,1,0:T(8,128)} %slice.341, f32[4,256,640]{2,1,0:T(8,128)} %slice.337, f32[4,256,640]{2,1,0:T(8,128)} %slice.339, f32[4,256,640]{2,1,0:T(8,128)} %slice.338), kind=kLoop, calls=%fused_computation.122 | loop fusion | flops 1966080 | bytes 15728640 | tf_op jit(solution)/shard_map/mul | solution.py:36
  162.1 14.1 %slice.336 = f32[4,255,640]{2,1,0:T(8,128)} slice(f32[4,512,640]{2,1,0:T(8,128)} %get-tuple-element.20), slice={[0:4:1], [2:512:2], [0:640:1]} | slice | bytes 5222400 | tf_op jit(solution)/shard_map/slice | solution.py:50
  176.2 7.5 %slice.347 = f32[4,128,640]{2,1,0:T(8,128)} slice(f32[4,256,640]{2,1,0:T(8,128)} %get-tuple-element.22), slice={[0:4:1], [0:255:2], [0:640:1]} | slice | bytes 2621440 | tf_op jit(solution)/shard_map/slice | solution.py:50
  183.7 7.5 %slice.343 = f32[4,128,640]{2,1,0:T(8,128)} slice(f32[4,256,640]{2,1,0:T(8,128)} %get-tuple-element.22), slice={[0:4:1], [1:256:2], [0:640:1]} | slice | bytes 2621440 | tf_op jit(solution)/shard_map/slice | solution.py:50
  191.2 7.6 %slice.342 = f32[4,127,640]{2,1,0:T(8,128)} slice(f32[4,256,640]{2,1,0:T(8,128)} %get-tuple-element.22), slice={[0:4:1], [2:256:2], [0:640:1]} | slice | bytes 2600960 | tf_op jit(solution)/shard_map/slice | solution.py:50
  238.6 5.4 %pad.72 = f32[4,256,640]{2,1,0:T(8,128)} pad(f32[4,128,640]{2,1,0:T(8,128)} %add.337, f32[]{:T(128)} %constant.61.clone.1), padding=0_0_0x1_0_1x0_0_0 | pad | bytes 3932164 | tf_op jit(solution)/shard_map/pad | solution.py:50
  250.2 6.6 %pad.73 = f32[4,512,640]{2,1,0:T(8,128)} pad(f32[4,256,640]{2,1,0:T(8,128)S(1)} %pad_maximum_fusion, f32[]{:T(128)} %constant.61.clone.1), padding=0_0_0x0_1_1x0_0_0 | pad | bytes 7864324 | tf_op jit(solution)/shard_map/pad | solution.py:50
  256.8 10.3 %pad.74 = f32[4,512,640]{2,1,0:T(8,128)} pad(f32[4,256,640]{2,1,0:T(8,128)} %add.339, f32[]{:T(128)} %constant.61.clone.1), padding=0_0_0x1_0_1x0_0_0 | pad | bytes 7864324 | tf_op jit(solution)/shard_map/pad | solution.py:50
  267.1 6.4 %multiply_reduce_fusion = (f32[4,512]{1,0:T(4,128)S(1)}, f32[4,512,640]{2,1,0:T(8,128)}) fusion(bf16[4,512,640]{2,1,0:T(8,128)(2,1)S(1)} %copy-done.4, f32[4,512,640]{2,1,0:T(8,128)} %pad.73, f32[4,512,640]{2,1,0:T(8,128)} %pad.74), kind=kLoop, calls=%fused_computation.7 | loop fusion | flops 10483712 | bytes 18358272 | tf_op jit(solution)/shard_map/reduce_sum | solution.py:52
  273.5 17.2 %all-gather.5 = f32[4,4,512]{2,1,0:T(4,128)S(1)} all-gather(f32[1,4,512]{2,1,0:T(4,128)S(1)} %bitcast.187), channel_id=4, replica_groups=mesh['time_0'=2,'time_1'=4,'time_2'=4,'time_3'=2,'chan'=4] {'chan'}, dimensions={0}, use_global_device_ids=true | all-gather | bytes 40960 | tf_op jit(solution)/shard_map/all_gather | solution.py:32
  290.8 4.5 %multiply_convert_fusion = bf16[4,512,640]{2,1,0:T(8,128)(2,1)} fusion(f32[4,512,640]{2,1,0:T(8,128)} %get-tuple-element.18, f32[640]{0:T(1024)S(1)} %copy-done.6, f32[4,512]{1,0:T(4,128)S(1)} %add_rsqrt_fusion), kind=kLoop, calls=%fused_computation.6 | loop fusion | flops 3932160 | bytes 7875072 | tf_op jit(solution)/shard_map/convert_element_type | solution.py:55
  (132 shorter events, 59.3 us)
Async XLA Ops:
  21.5 1.7 copy-start.2
  24.4 58.9 %copy-start = (f32[4,512,640]{2,1,0:T(8,128)}, f32[4,512,640]{2,1,0:T(8,128)S(1)}, u32[]{:S(2)}) copy-start(f32[4,512,640]{2,1,0:T(8,128)S(1)} %get-tuple-element.25) | copy-start | bytes 15728644
  218.0 3.5 %copy-start.3 = (f32[4,64,640]{2,1,0:T(8,128)S(1)}, f32[4,64,640]{2,1,0:T(8,128)}, u32[]{:S(2)}) copy-start(f32[4,64,640]{2,1,0:T(8,128)} %slice.353) | copy-start | bytes 1966084
  229.4 1.1 copy-start.5
  244.0 4.0 %copy-start.1 = (f32[4,256,640]{2,1,0:T(8,128)S(1)}, f32[4,256,640]{2,1,0:T(8,128)}, u32[]{:S(2)}) copy-start(f32[4,256,640]{2,1,0:T(8,128)} %pad.72) | copy-start | bytes 7864324
  256.8 10.3 %copy-start.4 = (bf16[4,512,640]{2,1,0:T(8,128)(2,1)S(1)}, bf16[4,512,640]{2,1,0:T(8,128)(2,1)}, u32[]{:S(2)}) copy-start(bf16[4,512,640]{2,1,0:T(8,128)(2,1)} %param.8) | copy-start | bytes 7864324
  267.1 23.7 %copy-start.6 = (f32[640]{0:T(1024)S(1)}, f32[640]{0:T(1024)}, u32[]{:S(2)}) copy-start(f32[640]{0:T(1024)} %param.9) | copy-start | bytes 7684
where the time goes:
time: 299 us; the launch traced here: 295 us
  local copies, waits for them, and re-layouts  162 us (54%)
  blocking collectives  77.6 us (26%)
  other arithmetic  55.2 us (18%)
    slice x52, local copies, waits for them, and re-layouts, body(): forward = lax.associative_scan(join_pair, (keep, started), axis=1)[1]  132 us
    all_gather x8, blocking collectives, entering(): pieces = jax.tree.map(lambda part: lax.all_gather(part, axis), so_far)  60.4 us
    pad x16, local copies, waits for them, and re-layouts, body(): forward = lax.associative_scan(join_pair, (keep, started), axis=1)[1]  26.1 us
    all_gather x1, blocking collectives, gathered_total(): return lax.all_gather(x, axis).sum(0)  17.2 us
    mul x10, other arithmetic, join_pair(): return (earlier[0] * later[0], later[0] * earlier[1] + later[1])  12 us
    another operation x3, other arithmetic  11.7 us
    reduce_sum x1, other arithmetic, body(): jnp.sum(steps, axis=1)  7.13 us
    reduce_sum x1, other arithmetic, body(): jnp.sum(gated * gated, axis=-1, keepdims=True)  6.4 us

commit v1 on v0

v1 whole, which is shorter than its diff:
```python
import jax
import jax.numpy as jnp
import numpy as np
from jax import lax
from jax.experimental import pallas as pl
from jax.experimental.pallas import tpu as pltpu
from jax.sharding import Mesh
from jax.sharding import PartitionSpec as P

TIME = ("time_0", "time_1", "time_2", "time_3")
CHIPS = ("time_0", "time_1", "time_2")
CORE = "time_3"
CHUNK = 256
SWAP = [(0, 1), (1, 0)]


def later_sums(decay, later_ref):
    return jnp.dot(later_ref[...], decay.astype(jnp.bfloat16), preferred_element_type=jnp.float32)


def summary_kernel(scale, decay_ref, drive_ref, later_ref, chunk_ref, total_ref):
    j = pl.program_id(1)
    decay = decay_ref[0]
    drive = drive_ref[0].astype(jnp.float32)
    pushed = jnp.sum(jnp.exp(later_sums(decay, later_ref)) * drive, axis=0, keepdims=True)
    lost = jnp.sum(decay, axis=0, keepdims=True) * scale
    chunk_ref[0, 0, 0:1] = lost
    chunk_ref[0, 0, 1:2] = pushed

    @pl.when(j == 0)
    def _():
        total_ref[0, 0:1] = lost
        total_ref[0, 1:2] = pushed

    @pl.when(j > 0)
    def _():
        total_ref[0, 0:1] = total_ref[0, 0:1] + lost
        total_ref[0, 1:2] = jnp.exp(-lost) * total_ref[0, 1:2] + pushed


def local_kernel(decay_ref, drive_ref, gate_ref, later_ref, upto_ref, after_ref, run_ref, open_ref):
    del after_ref
    logs = later_sums(decay_ref[0], later_ref)
    weight = jnp.exp(logs)
    drive = drive_ref[0]
    less = (drive.astype(jnp.float32) * (1.0 - weight)).astype(jnp.bfloat16)
    run_ref[0] = jnp.dot(upto_ref[...], drive, preferred_element_type=jnp.float32) - jnp.dot(
        upto_ref[...], less, preferred_element_type=jnp.float32
    )
    gate = 0.5 * jnp.tanh(0.5 * gate_ref[0].astype(jnp.float32)) + 0.5
    open_ref[0] = jnp.exp(-logs) * gate


def power_kernel(run_ref, open_ref, start_ref, chunk_ref, gated_ref, power_ref, carry_ref):
    j = pl.program_id(1)

    @pl.when(j == 0)
    def _():
        carry_ref[...] = start_ref[0]

    kept = carry_ref[...] * jnp.exp(-chunk_ref[0, 0, 0:1])
    gated = (run_ref[0] + kept) * open_ref[0]
    carry_ref[...] = kept + chunk_ref[0, 0, 1:2]
    gated_ref[0] = gated
    square = gated * gated
    lanes = sum(square[:, k * 128 : (k + 1) * 128] for k in range(square.shape[1] // 128))
    power_ref[0, 0] = jnp.sum(lanes.T, axis=0, keepdims=True)


def norm_kernel(channels, eps, gated_ref, power_ref, gain_ref, out_ref):
    rate = lax.rsqrt(power_ref[0, 0] * (1.0 / channels) + eps)
    rate = jnp.broadcast_to(rate, (128, rate.shape[1])).T
    gated = gated_ref[0]
    for k in range(gated.shape[1] // 128):
        at = slice(k * 128, (k + 1) * 128)
        out_ref[0, :, at] = (gated[:, at] * rate * gain_ref[:, at]).astype(jnp.bfloat16)


def params(mib):
    return pltpu.CompilerParams(
        dimension_semantics=("arbitrary", "arbitrary"), vmem_limit_bytes=mib * 1024 * 1024
    )


def join_pair(earlier, later):
    return (earlier[0] + later[0], jnp.exp(-later[0]) * earlier[1] + later[1])


def total_over_chan(x):
    x = x + lax.ppermute(x, "chan", [(i, i ^ 1) for i in range(4)])
    return x + lax.ppermute(x, "chan", [(i, i ^ 3) for i in range(4)])


def body(decay_rate, drive_in, gate_in, norm_gain):
    batch, length, width = decay_rate.shape
    total_length = length * lax.axis_size(TIME)
    channels = width * lax.axis_size("chan")
    chunks = length // CHUNK
    half = batch // 2
    row = np.arange(CHUNK)
    later = jnp.asarray((row[None, :] > row[:, None]) * (-1.0 / total_length), jnp.bfloat16)
    upto = jnp.asarray(row[None, :] <= row[:, None], jnp.bfloat16)
    grid = (batch, chunks)
    block = pl.BlockSpec((1, CHUNK, width), lambda b, j: (b, j, 0))
    square = pl.BlockSpec((CHUNK, CHUNK), lambda b, j: (0, 0))
    by_chunk = pl.BlockSpec((1, 1, 2, width), lambda b, j: (b, j, 0, 0))
    by_batch = pl.BlockSpec((1, 2, width), lambda b, j: (b, 0, 0))
    f32 = jnp.float32
    wide = jax.ShapeDtypeStruct((batch, length, width), f32)

    chunk, total = pl.pallas_call(
        lambda *refs: summary_kernel(1.0 / total_length, *refs),
        grid=grid,
        in_specs=[block, block, square],
        out_specs=[by_chunk, by_batch],
        out_shape=[
            jax.ShapeDtypeStruct((batch, chunks, 2, width), f32),
            jax.ShapeDtypeStruct((batch, 2, width), f32),
        ],
        compiler_params=params(12),
        name="summary",
    )(decay_rate, drive_in, later)

    core, chip = lax.axis_index(CORE), lax.axis_index(CHIPS)
    other = lax.ppermute(total, CORE, SWAP)
    first = jnp.where(core == 0, total, other)
    second = jnp.where(core == 0, other, total)
    lost, pushed = join_pair((first[:, 0], first[:, 1]), (second[:, 0], second[:, 1]))
    both = jnp.stack([lost, pushed])
    both = jnp.where(core == 0, both[:, :half], both[:, half:])
    peers = lax.axis_size(CHIPS)
    sent = jnp.broadcast_to(both, (peers,) + both.shape)
    pieces = lax.all_to_all(sent, CHIPS, 0, 0)

    run, opened = pl.pallas_call(
        local_kernel,
        grid=grid,
        in_specs=[block, block, block, square, square, pl.BlockSpec((1, 2, width), lambda b, j: (0, 0, 0))],
        out_specs=[block, block],
        out_shape=[wide, wide],
        compiler_params=params(16),
        cost_estimate=pl.CostEstimate(flops=4_000_000_000, transcendentals=0, bytes_accessed=20_000_000),
        name="local",
    )(decay_rate, drive_in, gate_in, later, upto, both)

    carry = jnp.zeros_like(both[0])
    for k in range(peers - 1):
        carry = jnp.where(k < chip, jnp.exp(-pieces[k, 0]) * carry + pieces[k, 1], carry)
    across = lax.ppermute(carry, CORE, SWAP)
    carry = jnp.where(
        core == 0, jnp.concatenate([carry, across]), jnp.concatenate([across, carry])
    )
    start = jnp.where(core == 0, carry, jnp.exp(-first[:, 0]) * carry + first[:, 1])

    gated, power = pl.pallas_call(
        power_kernel,
        grid=grid,
        in_specs=[block, block, pl.BlockSpec((1, 1, width), lambda b, j: (b, 0, 0)), by_chunk],
        out_specs=[block, pl.BlockSpec((1, 1, 1, CHUNK), lambda b, j: (b, j, 0, 0))],
        out_shape=[wide, jax.ShapeDtypeStruct((batch, chunks, 1, CHUNK), f32)],
        scratch_shapes=[pltpu.VMEM((1, width), f32)],
        compiler_params=params(12),
        name="power",
    )(run, opened, start[:, None], chunk)

    power = total_over_chan(power)

    return pl.pallas_call(
        lambda *refs: norm_kernel(channels, 1e-6 * total_length, *refs),
        grid=grid,
        in_specs=[
            block,
            pl.BlockSpec((1, 1, 1, CHUNK), lambda b, j: (b, j, 0, 0)),
            pl.BlockSpec((1, width), lambda b, j: (0, 0)),
        ],
        out_specs=block,
        out_shape=jax.ShapeDtypeStruct((batch, length, width), jnp.bfloat16),
        compiler_params=params(12),
        name="norm",
    )(gated, power, norm_gain[None])


def solution(mesh):
    split = Mesh(
        mesh.devices.reshape(2, 4, 4, 2, mesh.shape["chan"]),
        TIME + ("chan",),
    )
    in_specs = (P(None, TIME, "chan"), P(None, TIME, "chan"), P(None, TIME, "chan"), P("chan"))
    out_specs = P(None, TIME, "chan")
    return jax.shard_map(body, mesh=split, in_specs=in_specs, out_specs=out_specs, check_vma=False)
```

time: 299 us -> 55.6 us (0.19)
  local copies, waits for them, and re-layouts: 162 us -> 10.2 us
  blocking collectives: 77.6 us -> 0 us
  other arithmetic: 55.2 us -> 0.28 us
  starting transfers between devices: 0 us -> 17.6 us
  Pallas kernels: 0 us -> 13.4 us
  waiting for transfers between devices: 0 us -> 12.9 us
    slice x60 -> x0, local copies, waits for them, and re-layouts: 132 us -> none  [the longest x52 132 us: body(): forward = lax.associative_scan(join_pair, (keep, started), axis=1)[1]]
    all_gather x9 -> x0, blocking collectives: 77.6 us -> none  [the longest x8 60.4 us: entering(): pieces = jax.tree.map(lambda part: lax.all_gather(part, axis), so_far)]
    pad x16 -> x0, local copies, waits for them, and re-layouts: 26.1 us -> none  [body(): forward = lax.associative_scan(join_pair, (keep, started), axis=1)[1]]
    reduce_sum x4 -> x0, other arithmetic: 14.8 us -> none  [the longest x1 7.13 us: body(): jnp.sum(steps, axis=1)]
    pallas_call x0 -> x4, Pallas kernels: none -> 13.4 us  [the longest x1 5.56 us: body(): pl.pallas_call(local_kernel, grid=grid, in_specs=[block, block, block, sq...]
    mul x10 -> x0, other arithmetic: 12 us -> none  [join_pair(): return (earlier[0] * later[0], later[0] * earlier[1] + later[1])]
    another operation x3 -> x0, other arithmetic: 11.7 us -> none
    add x18 -> x3, other arithmetic: 10.6 us -> 0.06 us  [the longest x1 0.03 us: join_pair(): return (earlier[0] + later[0], jnp.exp(-later[0]) * earlier[1] + later[1])]
  transfers between devices with their start and end apart: 0 -> 5, of which waited for: 0 -> 4; matrix products, arithmetic and copies ran while one was open for 0% -> 0% of each run, Pallas kernels for 0% -> 10%
where the time goes in v1:
time: 55.6 us; the launch traced here: 54.6 us
  starting transfers between devices  17.6 us (32%)
  Pallas kernels  13.4 us (24%)
  waiting for transfers between devices  12.9 us (23%)
  local copies, waits for them, and re-layouts  10.2 us (18%)
    unnamed x18, local copies, waits for them, and re-layouts  9.37 us
    all_to_all x1, starting transfers between devices, body(): pieces = lax.all_to_all(sent, CHIPS, 0, 0)  8.97 us
    all_to_all x1, waiting for transfers between devices, body(): pieces = lax.all_to_all(sent, CHIPS, 0, 0)  8.45 us
    pallas_call x1, Pallas kernels, body(): pl.pallas_call(local_kernel, grid=grid, in_specs=[block, block, block, sq...  5.56 us
    ppermute x1, starting transfers between devices, total_over_chan(): return x + lax.ppermute(x, 'chan', [(i, i ^ 3) for i in range(4)])  5.14 us
    pallas_call x1, Pallas kernels, body(): pl.pallas_call(lambda *refs: norm_kernel(channels, 1e-06 * total_length,...  3.71 us
    ppermute x1, starting transfers between devices, total_over_chan(): x = x + lax.ppermute(x, 'chan', [(i, i ^ 1) for i in range(4)])  3.36 us
    pallas_call x1, Pallas kernels, body(): pl.pallas_call(lambda *refs: summary_kernel(1.0 / total_length, *refs), g...  2.53 us
  transfers between devices with their start and end apart: 5, of which 4 were waited for; matrix products, arithmetic and copies ran while one was open for 0% of the time, Pallas kernels for 10%

profile of v1, /device:TPU:2, one launch (start us, length us, event | category | flops | bytes accessed | tf_op | source)
XLA Modules:
  0.0 54.6 jit_solution(10823637859444337477)
XLA Ops:
  0.0 2.5 %copy-done = f32[4,512,640]{2,1,0:T(8,128)S(1)} copy-done((f32[4,512,640]{2,1,0:T(8,128)S(1)}, f32[4,512,640]{2,1,0:T(8,128)}, u32[]{:S(2)}) %copy-start) | copy-done | bytes 5242904
  2.5 1.7 %copy-done.2 = bf16[4,512,640]{2,1,0:T(8,128)(2,1)S(1)} copy-done((bf16[4,512,640]{2,1,0:T(8,128)(2,1)S(1)}, bf16[4,512,640]{2,1,0:T(8,128)(2,1)}, u32[]{:S(2)}) %copy-start.2) | copy-done | bytes 2621464
  4.2 0.9 %copy-done.4 = bf16[256,256]{1,0:T(8,128)(2,1)S(1)} copy-done((bf16[256,256]{1,0:T(8,128)(2,1)S(1)}, bf16[256,256]{1,0:T(8,128)(2,1)}, u32[]{:S(2)}) %copy-start.4) | copy-done | bytes 131096
  5.1 2.5 %summary.1 = (f32[4,2,2,640]{3,2,1,0:T(2,128)S(1)}, f32[4,2,640]{2,1,0:T(2,128)S(1)}) custom-call(f32[4,512,640]{2,1,0:T(8,128)S(1)} %copy-done, bf16[4,512,640]{2,1,0:T(8,128)(2,1)S(1)} %copy-done.2, bf16[256,256]{1,0:T(8,128)(2,1)S(1)} %copy-done.4), custom_call_target="tpu_custom_call" | custom-call | tf_op jit(solution)/shard_map/summary/pallas_call | solution.py:111
  7.7 0.1 collective-permute-start
  7.8 1.2 %collective-permute-done = f32[4,2,640]{2,1,0:T(2,128)S(1)} collective-permute-done((f32[4,2,640]{2,1,0:T(2,128)S(1)}, f32[4,2,640]{2,1,0:T(2,128)S(1)}, u32[]{:S(2)}, u32[]{:S(2)}) %collective-permute-start) | collective-permute-done | bytes 20512 | tf_op jit(solution)/shard_map/ppermute | solution.py:125
  9.0 0.8 %broadcast_in_dim.12 = f32[32,2,2,640]{3,2,1,0:T(2,128)} broadcast(f32[2,2,640]{2,1,0:T(2,128)S(1)} %copy.7.after_ref), dimensions={1,2,3} | broadcast | bytes 337920 | tf_op jit(solution)/shard_map/broadcast_in_dim | solution.py:132
  9.9 9.0 %all-to-all-start = ((f32[32,2,2,640]{3,2,1,0:T(2,128)}), f32[32,2,2,640]{3,2,1,0:T(2,128)S(1)}, u32[]{:S(2)}, u32[]{:S(2)}) async-start(f32[32,2,2,640]{3,2,1,0:T(2,128)} %broadcast_in_dim.12), calls=%async_computation | async-start | bytes 655360 | tf_op jit(solution)/shard_map/all_to_all | solution.py:133
  18.9 8.4 %all-to-all-done = f32[32,2,2,640]{3,2,1,0:T(2,128)S(1)} async-done(((f32[32,2,2,640]{3,2,1,0:T(2,128)}), f32[32,2,2,640]{3,2,1,0:T(2,128)S(1)}, u32[]{:S(2)}, u32[]{:S(2)}) %all-to-all-start) | async-done | bytes 327712 | tf_op jit(solution)/shard_map/all_to_all | solution.py:133
  27.3 0.2 fusion.4
  27.5 0.1 collective-permute-start.1
  27.6 0.0 copy-start.1
  27.7 2.5 %copy-done.1 = f32[4,512,640]{2,1,0:T(8,128)S(1)} copy-done((f32[4,512,640]{2,1,0:T(8,128)S(1)}, f32[4,512,640]{2,1,0:T(8,128)}, u32[]{:S(2)}) %copy-start.1) | copy-done | bytes 5242904
  30.1 1.7 %copy-done.6 = bf16[4,512,640]{2,1,0:T(8,128)(2,1)S(1)} copy-done((bf16[4,512,640]{2,1,0:T(8,128)(2,1)S(1)}, bf16[4,512,640]{2,1,0:T(8,128)(2,1)}, u32[]{:S(2)}) %copy-start.6) | copy-done | bytes 2621464
  31.9 5.6 %local.1 = (f32[4,512,640]{2,1,0:T(8,128)S(1)}, f32[4,512,640]{2,1,0:T(8,128)S(1)}) custom-call(f32[4,512,640]{2,1,0:T(8,128)S(1)} %copy-done.1, bf16[4,512,640]{2,1,0:T(8,128)(2,1)S(1)} %copy-done.3, bf16[4,512,640]{2,1,0:T(8,128)(2,1)S(1)} %copy-done.6, bf16[256,256]{1,0:T(8,128)(2,1)S(1)} %copy-done.5, bf16[256,256]{1,0:T(8,128)(2,1)S(1)} %copy-done.7, ...), custom_call_target="tpu_custom_call" | custom-call | flops 4000000000 | bytes 20000000 | tf_op jit(solution)/shard_map/local/pallas_call | solution.py:135
  37.5 0.0 collective-permute-done.1
  37.5 0.0 copy-start.8
  37.5 1.6 %power.1 = (f32[4,512,640]{2,1,0:T(8,128)S(1)}, f32[4,2,1,256]{3,2,1,0:T(1,128)S(1)}) custom-call(f32[4,512,640]{2,1,0:T(8,128)S(1)} %get-tuple-element.12.run_ref, f32[4,512,640]{2,1,0:T(8,128)S(1)} %get-tuple-element.13.open_ref, f32[4,1,640]{2,1,0:T(1,128)S(1)} %broadcast_select_fusion.start_ref, f32[4,2,2,640]{3,2,1,0:T(2,128)S(1)} %get-tuple-element.14.chunk_ref), custom_call_target="tpu_custom_call" | custom-call | tf_op jit(solution)/shard_map/power/pallas_call | solution.py:155
  39.1 3.4 %collective-permute-start.2 = (f32[4,2,1,256]{3,2,1,0:T(1,128)S(1)}, f32[4,2,1,256]{3,2,1,0:T(1,128)S(1)}, u32[]{:S(2)}, u32[]{:S(2)}) collective-permute-start(f32[4,2,1,256]{3,2,1,0:T(1,128)S(1)} %get-tuple-element.16), channel_id=1, source_target_pairs={{0,1},{1,0},{2,3},{3,2},{4,5},{5,4},{6,7},{7,6},{8,9},{9,8},{10,11... | collective-permute-start | bytes 24584 | tf_op jit(solution)/shard_map/ppermute | solution.py:90
  42.5 1.6 %collective-permute-done.2 = f32[4,2,1,256]{3,2,1,0:T(1,128)S(1)} collective-permute-done((f32[4,2,1,256]{3,2,1,0:T(1,128)S(1)}, f32[4,2,1,256]{3,2,1,0:T(1,128)S(1)}, u32[]{:S(2)}, u32[]{:S(2)}) %collective-permute-start.2) | collective-permute-done | bytes 8224 | tf_op jit(solution)/shard_map/ppermute | solution.py:90
  44.1 5.1 %collective-permute-start.3 = (f32[4,2,1,256]{3,2,1,0:T(1,128)S(1)}, f32[4,2,1,256]{3,2,1,0:T(1,128)S(1)}, u32[]{:S(2)}, u32[]{:S(2)}) collective-permute-start(f32[4,2,1,256]{3,2,1,0:T(1,128)S(1)} %add.456), channel_id=1, source_target_pairs={{0,3},{1,2},{2,1},{3,0},{4,7},{5,6},{6,5},{7,4},{8,11},{9,10},{10,... | collective-permute-start | bytes 24584 | tf_op jit(solution)/shard_map/ppermute | solution.py:91
  49.3 0.0 copy-done.8
  49.3 1.6 %collective-permute-done.3 = f32[4,2,1,256]{3,2,1,0:T(1,128)S(1)} collective-permute-done((f32[4,2,1,256]{3,2,1,0:T(1,128)S(1)}, f32[4,2,1,256]{3,2,1,0:T(1,128)S(1)}, u32[]{:S(2)}, u32[]{:S(2)}) %collective-permute-start.3) | collective-permute-done | bytes 8224 | tf_op jit(solution)/shard_map/ppermute | solution.py:91
  50.9 3.7 %norm.1 = bf16[4,512,640]{2,1,0:T(8,128)(2,1)} custom-call(f32[4,512,640]{2,1,0:T(8,128)S(1)} %get-tuple-element.15.refs_0_, f32[4,2,1,256]{3,2,1,0:T(1,128)S(1)} %add.457.refs_1_, f32[1,640]{1,0:T(1,128)S(1)} %broadcast_in_dim.15.refs_2_), custom_call_target="tpu_custom_call" | custom-call | tf_op jit(solution)/shard_map/norm/pallas_call | solution.py:168
  (20 shorter events, 0.2 us)
Async XLA Ops:
  0.0 2.5 %copy-start = (f32[4,512,640]{2,1,0:T(8,128)S(1)}, f32[4,512,640]{2,1,0:T(8,128)}, u32[]{:S(2)}) copy-start(f32[4,512,640]{2,1,0:T(8,128)} %decay_ref.1) | copy-start | bytes 15728644
  2.5 1.7 %copy-start.2 = (bf16[4,512,640]{2,1,0:T(8,128)(2,1)S(1)}, bf16[4,512,640]{2,1,0:T(8,128)(2,1)}, u32[]{:S(2)}) copy-start(bf16[4,512,640]{2,1,0:T(8,128)(2,1)} %drive_ref.1) | copy-start | bytes 7864324
  4.2 0.9 %copy-start.4 = (bf16[256,256]{1,0:T(8,128)(2,1)S(1)}, bf16[256,256]{1,0:T(8,128)(2,1)}, u32[]{:S(2)}) copy-start(bf16[256,256]{1,0:T(8,128)(2,1)} %constant.86.clone.refs_2_.later_ref) | copy-start | bytes 393220
  5.1 22.5 %copy-start.3 = (bf16[4,512,640]{2,1,0:T(8,128)(2,1)S(1)}, bf16[4,512,640]{2,1,0:T(8,128)(2,1)}, u32[]{:S(2)}) copy-start(bf16[4,512,640]{2,1,0:T(8,128)(2,1)} %drive_ref.1) | copy-start | bytes 7864324
  5.1 22.5 %copy-start.5 = (bf16[256,256]{1,0:T(8,128)(2,1)S(1)}, bf16[256,256]{1,0:T(8,128)(2,1)}, u32[]{:S(2)}) copy-start(bf16[256,256]{1,0:T(8,128)(2,1)} %constant.86.clone.refs_2_.later_ref) | copy-start | bytes 393220
  5.1 22.5 %copy-start.7 = (bf16[256,256]{1,0:T(8,128)(2,1)S(1)}, bf16[256,256]{1,0:T(8,128)(2,1)}, u32[]{:S(2)}) copy-start(bf16[256,256]{1,0:T(8,128)(2,1)} %constant.87.clone.upto_ref) | copy-start | bytes 393220
  7.7 1.3 %collective-permute-start = (f32[4,2,640]{2,1,0:T(2,128)S(1)}, f32[4,2,640]{2,1,0:T(2,128)S(1)}, u32[]{:S(2)}, u32[]{:S(2)}) collective-permute-start(f32[4,2,640]{2,1,0:T(2,128)S(1)} %get-tuple-element.11), channel_id=1, source_target_pairs={{0,4},{4,0},{1,5},{5,1},{2,6},{6,2},{3,7},{7,3},{8,12},{12,8},{9,1... | collective-permute-start | bytes 61448 | tf_op jit(solution)/shard_map/ppermute | solution.py:125
  9.9 17.5 %all-to-all-start = ((f32[32,2,2,640]{3,2,1,0:T(2,128)}), f32[32,2,2,640]{3,2,1,0:T(2,128)S(1)}, u32[]{:S(2)}, u32[]{:S(2)}) async-start(f32[32,2,2,640]{3,2,1,0:T(2,128)} %broadcast_in_dim.12), calls=%async_computation | async-start | bytes 655360 | tf_op jit(solution)/shard_map/all_to_all | solution.py:133
  27.5 9.9 %collective-permute-start.1 = (f32[2,640]{1,0:T(2,128)S(1)}, f32[2,640]{1,0:T(2,128)S(1)}, u32[]{:S(2)}, u32[]{:S(2)}) collective-permute-start(f32[2,640]{1,0:T(2,128)S(1)} %fusion.4), channel_id=1, source_target_pairs={{0,4},{4,0},{1,5},{5,1},{2,6},{6,2},{3,7},{7,3},{8,12},{12,8},{9,1... | collective-permute-start | bytes 15368 | tf_op jit(solution)/shard_map/ppermute | solution.py:149
  27.6 2.5 %copy-start.1 = (f32[4,512,640]{2,1,0:T(8,128)S(1)}, f32[4,512,640]{2,1,0:T(8,128)}, u32[]{:S(2)}) copy-start(f32[4,512,640]{2,1,0:T(8,128)} %decay_ref.1) | copy-start | bytes 15728644
  30.1 1.7 %copy-start.6 = (bf16[4,512,640]{2,1,0:T(8,128)(2,1)S(1)}, bf16[4,512,640]{2,1,0:T(8,128)(2,1)}, u32[]{:S(2)}) copy-start(bf16[4,512,640]{2,1,0:T(8,128)(2,1)} %gate_ref.1) | copy-start | bytes 7864324
  37.5 11.7 %copy-start.8 = (f32[640]{0:T(1024)S(1)}, f32[640]{0:T(1024)}, u32[]{:S(2)}) copy-start(f32[640]{0:T(1024)} %param.9) | copy-start | bytes 7684
  39.1 5.0 %collective-permute-start.2 = (f32[4,2,1,256]{3,2,1,0:T(1,128)S(1)}, f32[4,2,1,256]{3,2,1,0:T(1,128)S(1)}, u32[]{:S(2)}, u32[]{:S(2)}) collective-permute-start(f32[4,2,1,256]{3,2,1,0:T(1,128)S(1)} %get-tuple-element.16), channel_id=1, source_target_pairs={{0,1},{1,0},{2,3},{3,2},{4,5},{5,4},{6,7},{7,6},{8,9},{9,8},{10,11... | collective-permute-start | bytes 24584 | tf_op jit(solution)/shard_map/ppermute | solution.py:90
  44.1 6.8 %collective-permute-start.3 = (f32[4,2,1,256]{3,2,1,0:T(1,128)S(1)}, f32[4,2,1,256]{3,2,1,0:T(1,128)S(1)}, u32[]{:S(2)}, u32[]{:S(2)}) collective-permute-start(f32[4,2,1,256]{3,2,1,0:T(1,128)S(1)} %add.456), channel_id=1, source_target_pairs={{0,3},{1,2},{2,1},{3,0},{4,7},{5,6},{6,5},{7,4},{8,11},{9,10},{10,... | collective-permute-start | bytes 24584 | tf_op jit(solution)/shard_map/ppermute | solution.py:91

commit v2 on v0

v2 whole, which is shorter than its diff:
```python
import jax
import jax.numpy as jnp
from jax import lax
from jax.experimental import pallas as pl
from jax.experimental.pallas import tpu as pltpu
from jax.sharding import Mesh
from jax.sharding import PartitionSpec as P

TIME = ("time_0", "time_1", "time_2", "time_3")
CHIPS = ("time_0", "time_1", "time_2")
CORE = "time_3"
CHUNK = 256
SWAP = [(0, 1), (1, 0)]
VMEM_LOCAL, VMEM_POWER, VMEM_NORM = 24, 8, 8


def columns(width):
    return [slice(k, min(k + 256, width)) for k in range(0, width, 256)]


def local_kernel(
    scale, place_ref, decay_hbm, drive_hbm, gate_hbm, chunk_ref, total_ref, run_ref, open_ref,
    decay_ref, drive_ref, gate_ref, later_ref, upto_ref, sems,
):
    del place_ref
    batch, length, width = decay_ref.shape
    chunks = length // CHUNK

    def loads(b, j):
        at = pl.ds(j * CHUNK, CHUNK)
        pairs = ((decay_hbm, decay_ref), (drive_hbm, drive_ref), (gate_hbm, gate_ref))
        return [
            pltpu.make_async_copy(hbm.at[b, at], ref.at[b, at], sems.at[k, b, j])
            for k, (hbm, ref) in enumerate(pairs)
        ]

    for b in range(batch):
        for j in range(chunks):
            for copy in loads(b, j):
                copy.start()

    row = lax.broadcasted_iota(jnp.int32, (CHUNK, CHUNK), 0)
    col = lax.broadcasted_iota(jnp.int32, (CHUNK, CHUNK), 1)
    later_ref[...] = jnp.where(col > row, -scale, 0.0).astype(jnp.bfloat16)
    upto_ref[...] = jnp.where(col > row, 0.0, 1.0).astype(jnp.bfloat16)
    f32 = jnp.float32

    @pl.loop(0, batch)
    def _(b):
        for j in range(chunks):
            for copy in loads(b, j):
                copy.wait()
            at = slice(j * CHUNK, (j + 1) * CHUNK)
            for cols in columns(width):
                decay = decay_ref[b, at, cols]
                drive = drive_ref[b, at, cols]
                wide = drive.astype(f32)
                logs = jnp.dot(later_ref[...], decay.astype(jnp.bfloat16), preferred_element_type=f32)
                weight = jnp.exp(logs)
                pushed = weight * wide
                less = (wide - pushed).astype(jnp.bfloat16)
                run_ref[b, at, cols] = jnp.dot(
                    upto_ref[...], drive, preferred_element_type=f32
                ) - jnp.dot(upto_ref[...], less, preferred_element_type=f32)
                gate = 0.5 * jnp.tanh(0.5 * gate_ref[b, at, cols].astype(f32)) + 0.5
                open_ref[b, at, cols] = jnp.exp(-logs) * gate
                pushed = jnp.sum(pushed, axis=0, keepdims=True)
                lost = jnp.sum(decay, axis=0, keepdims=True) * scale
                chunk_ref[b, j, 0:1, cols] = lost
                chunk_ref[b, j, 1:2, cols] = pushed
                if j == 0:
                    total_ref[b, 0:1, cols] = lost
                    total_ref[b, 1:2, cols] = pushed
                else:
                    total_ref[b, 0:1, cols] = total_ref[b, 0:1, cols] + lost
                    total_ref[b, 1:2, cols] = jnp.exp(-lost) * total_ref[b, 1:2, cols] + pushed


def pack_kernel(place_ref, total_ref, other_ref, sent_ref):
    core = place_ref[0] % 2
    batch = total_ref.shape[0]

    def half(begin, first_ref, second_ref):
        for b in range(batch // 2):
            at = begin + b
            lost = second_ref[at, 0:1]
            pushed = jnp.exp(-lost) * first_ref[at, 1:2] + second_ref[at, 1:2]
            lost = lost + first_ref[at, 0:1]
            for k in range(sent_ref.shape[0]):
                sent_ref[k, 0, b : b + 1] = lost
                sent_ref[k, 1, b : b + 1] = pushed

    @pl.when(core == 0)
    def _():
        half(0, total_ref, other_ref)

    @pl.when(core == 1)
    def _():
        half(batch // 2, other_ref, total_ref)


def carry_kernel(place_ref, pieces_ref, carry_ref):
    chip = place_ref[0] // 2
    carry = jnp.zeros(carry_ref.shape, jnp.float32)
    for k in range(pieces_ref.shape[0] - 1):
        passed = jnp.exp(-pieces_ref[k, 0]) * carry + pieces_ref[k, 1]
        carry = jnp.where(k < chip, passed, carry)
    carry_ref[...] = carry


def power_kernel(
    place_ref, run_ref, open_ref, chunk_ref, mine_ref, across_ref, other_ref,
    gated_ref, power_ref, start_ref,
):
    batch, length, width = run_ref.shape
    core = place_ref[0] % 2
    for b in range(batch):
        h, at = divmod(b, batch // 2)
        carry = jnp.where(core == h, mine_ref[at : at + 1], across_ref[at : at + 1])
        passed = jnp.exp(-other_ref[b, 0:1]) * carry + other_ref[b, 1:2]
        start_ref[b] = jnp.where(core == 0, carry, passed)

    @pl.loop(0, batch)
    def _(b):
        carry = start_ref[b]
        for j in range(length // CHUNK):
            at = slice(j * CHUNK, (j + 1) * CHUNK)
            kept = carry * jnp.exp(-chunk_ref[b, j, 0:1])
            carry = kept + chunk_ref[b, j, 1:2]
            lanes = jnp.zeros((CHUNK, 128), jnp.float32)
            for k in range(width // 128):
                cols = slice(k * 128, (k + 1) * 128)
                gated = (run_ref[b, at, cols] + kept[:, cols]) * open_ref[b, at, cols]
                gated_ref[b, at, cols] = gated
                lanes = lanes + gated * gated
            power_ref[b, j] = jnp.sum(lanes.T, axis=0, keepdims=True)


def norm_kernel(channels, eps, gated_ref, power_ref, gain_ref, out_hbm, out_ref, sems):
    batch, length, width = gated_ref.shape
    chunks = length // CHUNK

    def store(b, j):
        at = pl.ds(j * CHUNK, CHUNK)
        return pltpu.make_async_copy(out_ref.at[b, at], out_hbm.at[b, at], sems.at[b, j])

    @pl.loop(0, batch)
    def _(b):
        for j in range(chunks):
            at = slice(j * CHUNK, (j + 1) * CHUNK)
            rate = lax.rsqrt(power_ref[b, j] * (1.0 / channels) + eps)
            rate = jnp.broadcast_to(rate, (128, CHUNK)).T
            for k in range(width // 128):
                cols = slice(k * 128, (k + 1) * 128)
                out = gated_ref[b, at, cols] * rate * gain_ref[:, cols]
                out_ref[b, at, cols] = out.astype(jnp.bfloat16)
            store(b, j).start()

    for b in range(batch):
        for j in range(chunks):
            store(b, j).wait()


def params(mib):
    return pltpu.CompilerParams(vmem_limit_bytes=mib * 1024 * 1024)


def total_over_chan(x):
    x = x + lax.ppermute(x, "chan", [(i, i ^ 1) for i in range(4)])
    return x + lax.ppermute(x, "chan", [(i, i ^ 3) for i in range(4)])


def body(decay_rate, drive_in, gate_in, norm_gain):
    batch, length, width = decay_rate.shape
    total_length = length * lax.axis_size(TIME)
    channels = width * lax.axis_size("chan")
    chunks = length // CHUNK
    f32 = jnp.float32
    shape = (batch, length, width)
    hbm = pl.BlockSpec(memory_space=pltpu.HBM)
    vmem = pl.BlockSpec(memory_space=pltpu.VMEM)

    place = lax.axis_index(TIME).astype(jnp.int32).reshape(1)
    smem = pl.BlockSpec(memory_space=pltpu.SMEM)

    chunk, total, run, opened = pl.pallas_call(
        lambda *refs: local_kernel(1.0 / total_length, *refs),
        in_specs=[smem, hbm, hbm, hbm],
        out_specs=[vmem] * 4,
        out_shape=[
            jax.ShapeDtypeStruct((batch, chunks, 2, width), f32),
            jax.ShapeDtypeStruct((batch, 2, width), f32),
            jax.ShapeDtypeStruct(shape, f32),
            jax.ShapeDtypeStruct(shape, f32),
        ],
        scratch_shapes=[
            pltpu.VMEM(shape, f32),
            pltpu.VMEM(shape, jnp.bfloat16),
            pltpu.VMEM(shape, jnp.bfloat16),
            pltpu.VMEM((CHUNK, CHUNK), jnp.bfloat16),
            pltpu.VMEM((CHUNK, CHUNK), jnp.bfloat16),
            pltpu.SemaphoreType.DMA((3, batch, chunks)),
        ],
        compiler_params=params(VMEM_LOCAL),
        name="local",
    )(place, *(pltpu.with_memory_space_constraint(x, pltpu.HBM) for x in (decay_rate, drive_in, gate_in)))

    peers = lax.axis_size(CHIPS)
    other = lax.ppermute(total, CORE, SWAP)
    sent = pl.pallas_call(
        pack_kernel,
        in_specs=[smem, vmem, vmem],
        out_specs=vmem,
        out_shape=jax.ShapeDtypeStruct((peers, 2, batch // 2, width), f32),
        compiler_params=params(4),
        name="pack",
    )(place, total, other)
    pieces = lax.all_to_all(sent, CHIPS, 0, 0)
    carry = pl.pallas_call(
        carry_kernel,
        in_specs=[smem, vmem],
        out_specs=vmem,
        out_shape=jax.ShapeDtypeStruct((batch // 2, width), f32),
        compiler_params=params(4),
        name="carry",
    )(place, pieces)
    across = lax.ppermute(carry, CORE, SWAP)

    gated, power = pl.pallas_call(
        power_kernel,
        in_specs=[smem] + [vmem] * 6,
        out_specs=[vmem] * 2,
        out_shape=[
            jax.ShapeDtypeStruct(shape, f32),
            jax.ShapeDtypeStruct((batch, chunks, 1, CHUNK), f32),
        ],
        scratch_shapes=[pltpu.VMEM((batch, 1, width), f32)],
        compiler_params=params(VMEM_POWER),
        name="power",
    )(place, run, opened, chunk, carry, across, other)

    power = total_over_chan(power)

    return pl.pallas_call(
        lambda *refs: norm_kernel(channels, 1e-6 * total_length, *refs),
        in_specs=[vmem] * 3,
        out_specs=hbm,
        out_shape=jax.ShapeDtypeStruct(shape, jnp.bfloat16),
        scratch_shapes=[pltpu.VMEM(shape, jnp.bfloat16), pltpu.SemaphoreType.DMA((batch, chunks))],
        compiler_params=params(VMEM_NORM),
        name="norm",
    )(gated, power, norm_gain[None])


def solution(mesh):
    split = Mesh(
        mesh.devices.reshape(2, 4, 4, 2, mesh.shape["chan"]),
        TIME + ("chan",),
    )
    in_specs = (P(None, TIME, "chan"), P(None, TIME, "chan"), P(None, TIME, "chan"), P("chan"))
    out_specs = P(None, TIME, "chan")
    return jax.shard_map(body, mesh=split, in_specs=in_specs, out_specs=out_specs, check_vma=False)
```

time: 299 us -> 43.6 us (0.15); the launches traced: 295 us -> 43.2 us
  local copies, waits for them, and re-layouts: 162 us -> 0.01 us
  blocking collectives: 77.6 us -> 17.3 us
  other arithmetic: 55.2 us -> 0.02 us
  Pallas kernels: 0 us -> 11.5 us
  starting transfers between devices: 0 us -> 8.68 us
  waiting for transfers between devices: 0 us -> 5.59 us
    slice x60 -> x0, local copies, waits for them, and re-layouts: 132 us -> none  [the longest x52 132 us: body(): forward = lax.associative_scan(join_pair, (keep, started), axis=1)[1]]
    all_gather x9 -> x0, blocking collectives: 77.6 us -> none  [the longest x8 60.4 us: entering(): pieces = jax.tree.map(lambda part: lax.all_gather(part, axis), so_far)]
    pad x16 -> x0, local copies, waits for them, and re-layouts: 26.1 us -> none  [body(): forward = lax.associative_scan(join_pair, (keep, started), axis=1)[1]]
    all_to_all x0 -> x1, blocking collectives: none -> 17.3 us  [body(): pieces = lax.all_to_all(sent, CHIPS, 0, 0)]
    reduce_sum x4 -> x0, other arithmetic: 14.8 us -> none  [the longest x1 7.13 us: body(): jnp.sum(steps, axis=1)]
    mul x10 -> x0, other arithmetic: 12 us -> none  [join_pair(): return (earlier[0] * later[0], later[0] * earlier[1] + later[1])]
    another operation x3 -> x0, other arithmetic: 11.7 us -> none
    pallas_call x0 -> x5, Pallas kernels: none -> 11.5 us  [the longest x1 8.54 us: body(): pl.pallas_call(lambda *refs: local_kernel(1.0 / total_length, *refs), in_...]
  transfers between devices with their start and end apart: 0 -> 4, of which waited for: 0 -> 4; matrix products, arithmetic and copies ran while one was open for 0% -> 0% of each run, Pallas kernels for 0% -> 0%
where the time goes in v2:
time: 43.6 us; the launch traced here: 43.2 us
  blocking collectives  17.3 us (40%)
  Pallas kernels  11.5 us (26%)
  starting transfers between devices  8.68 us (20%)
  waiting for transfers between devices  5.59 us (13%)
    all_to_all x1, blocking collectives, body(): pieces = lax.all_to_all(sent, CHIPS, 0, 0)  17.3 us
    pallas_call x1, Pallas kernels, body(): pl.pallas_call(lambda *refs: local_kernel(1.0 / total_length, *refs), in_...  8.54 us
    ppermute x1, starting transfers between devices, total_over_chan(): return x + lax.ppermute(x, 'chan', [(i, i ^ 3) for i in range(4)])  5.14 us
    ppermute x1, starting transfers between devices, total_over_chan(): x = x + lax.ppermute(x, 'chan', [(i, i ^ 1) for i in range(4)])  3.36 us
    pallas_call x1, Pallas kernels, body(): pl.pallas_call(lambda *refs: norm_kernel(channels, 1e-06 * total_length,...  1.74 us
    ppermute x1, waiting for transfers between devices, total_over_chan(): x = x + lax.ppermute(x, 'chan', [(i, i ^ 1) for i in range(4)])  1.63 us
    ppermute x1, waiting for transfers between devices, total_over_chan(): return x + lax.ppermute(x, 'chan', [(i, i ^ 3) for i in range(4)])  1.62 us
    ppermute x1, waiting for transfers between devices, body(): other = lax.ppermute(total, CORE, SWAP)  1.18 us
  transfers between devices with their start and end apart: 4, of which 4 were waited for; matrix products, arithmetic and copies ran while one was open for 0% of the time, Pallas kernels for 0%

profile of v2, /device:TPU:2, one launch (start us, length us, event | category | flops | bytes accessed | tf_op | source)
XLA Modules:
  0.0 43.2 jit_solution(16161673295157815839)
XLA Ops:
  0.0 8.5 %local.1 = (f32[4,2,2,640]{3,2,1,0:T(2,128)S(1)}, f32[4,2,640]{2,1,0:T(2,128)S(1)}, f32[4,512,640]{2,1,0:T(8,128)S(1)}, f32[4,512,640]{2,1,0:T(8,128)S(1)}) custom-call(s32[1]{0:T(128)} %bitcast.refs_0_.place_ref, f32[4,512,640]{2,1,0:T(8,128)} %refs_1_.1, bf16[4,512,640]{2,1,0:T(8,128)(2,1)} %refs_2_.1, bf16[4,512,640]{2,1,0:T(8,128)(2,1)} %refs_3_.1), custom_call_target="tpu_custom_call" | custom-call | tf_op jit(solution)/shard_map/local/pallas_call | solution.py:186
  8.6 0.1 collective-permute-start
  8.7 1.2 %collective-permute-done.other_ref = f32[4,2,640]{2,1,0:T(2,128)S(1)} collective-permute-done((f32[4,2,640]{2,1,0:T(2,128)S(1)}, f32[4,2,640]{2,1,0:T(2,128)S(1)}, u32[]{:S(2)}, u32[]{:S(2)}) %collective-permute-start) | collective-permute-done | bytes 20512 | tf_op jit(solution)/shard_map/ppermute | solution.py:209
  9.9 17.3 %all_to_all.5.pieces_ref = f32[32,2,2,640]{3,2,1,0:T(2,128)S(1)} all-to-all(f32[32,2,2,640]{3,2,1,0:T(2,128)S(1)} %pack.1), channel_id=1, replica_groups=mesh['time_0'=2,'time_1'=4,'time_2'=4,'time_3'=2,'chan'=4] {'time_0','ti..., dimensions={0} | all-to-all | bytes 655360 | tf_op jit(solution)/shard_map/all_to_all | solution.py:218
  27.2 0.1 carry.1.mine_ref
  27.3 0.1 collective-permute-start.1
  27.4 1.2 %collective-permute-done.1.across_ref = f32[2,640]{1,0:T(2,128)S(1)} collective-permute-done((f32[2,640]{1,0:T(2,128)S(1)}, f32[2,640]{1,0:T(2,128)S(1)}, u32[]{:S(2)}, u32[]{:S(2)}) %collective-permute-start.1) | collective-permute-done | bytes 5152 | tf_op jit(solution)/shard_map/ppermute | solution.py:227
  28.5 0.0 copy-start
  28.5 1.1 %power.1 = (f32[4,512,640]{2,1,0:T(8,128)S(1)}, f32[4,2,1,256]{3,2,1,0:T(1,128)S(1)}) custom-call(s32[1]{0:T(128)} %bitcast.refs_0_.place_ref, f32[4,512,640]{2,1,0:T(8,128)S(1)} %get-tuple-element.11.run_ref, f32[4,512,640]{2,1,0:T(8,128)S(1)} %get-tuple-element.12.open_ref, f32[4,2,2,640]{3,2,1,0:T(2,128)S(1)} %get-tuple-element.13.chunk_ref, ...), custom_call_target="tpu_custom_call" | custom-call | tf_op jit(solution)/shard_map/power/pallas_call | solution.py:229
  29.6 3.4 %collective-permute-start.2 = (f32[4,2,1,256]{3,2,1,0:T(1,128)S(1)}, f32[4,2,1,256]{3,2,1,0:T(1,128)S(1)}, u32[]{:S(2)}, u32[]{:S(2)}) collective-permute-start(f32[4,2,1,256]{3,2,1,0:T(1,128)S(1)} %get-tuple-element.16), channel_id=1, source_target_pairs={{0,1},{1,0},{2,3},{3,2},{4,5},{5,4},{6,7},{7,6},{8,9},{9,8},{10,11... | collective-permute-start | bytes 24584 | tf_op jit(solution)/shard_map/ppermute | solution.py:169
  33.0 1.6 %collective-permute-done.2 = f32[4,2,1,256]{3,2,1,0:T(1,128)S(1)} collective-permute-done((f32[4,2,1,256]{3,2,1,0:T(1,128)S(1)}, f32[4,2,1,256]{3,2,1,0:T(1,128)S(1)}, u32[]{:S(2)}, u32[]{:S(2)}) %collective-permute-start.2) | collective-permute-done | bytes 8224 | tf_op jit(solution)/shard_map/ppermute | solution.py:169
  34.6 5.1 %collective-permute-start.3 = (f32[4,2,1,256]{3,2,1,0:T(1,128)S(1)}, f32[4,2,1,256]{3,2,1,0:T(1,128)S(1)}, u32[]{:S(2)}, u32[]{:S(2)}) collective-permute-start(f32[4,2,1,256]{3,2,1,0:T(1,128)S(1)} %add.18), channel_id=1, source_target_pairs={{0,3},{1,2},{2,1},{3,0},{4,7},{5,6},{6,5},{7,4},{8,11},{9,10},{10,... | collective-permute-start | bytes 24584 | tf_op jit(solution)/shard_map/ppermute | solution.py:170
  39.8 0.0 copy-done
  39.8 1.6 %collective-permute-done.3 = f32[4,2,1,256]{3,2,1,0:T(1,128)S(1)} collective-permute-done((f32[4,2,1,256]{3,2,1,0:T(1,128)S(1)}, f32[4,2,1,256]{3,2,1,0:T(1,128)S(1)}, u32[]{:S(2)}, u32[]{:S(2)}) %collective-permute-start.3) | collective-permute-done | bytes 8224 | tf_op jit(solution)/shard_map/ppermute | solution.py:170
  41.4 1.7 %norm.1 = bf16[4,512,640]{2,1,0:T(8,128)(2,1)} custom-call(f32[4,512,640]{2,1,0:T(8,128)S(1)} %get-tuple-element.15.refs_0_, f32[4,2,1,256]{3,2,1,0:T(1,128)S(1)} %add.19.refs_1_, f32[1,640]{1,0:T(1,128)S(1)} %broadcast_in_dim.3.refs_2_), custom_call_target="tpu_custom_call" | custom-call | tf_op jit(solution)/shard_map/norm/pallas_call | solution.py:244
  (4 shorter events, 0.1 us)
Async XLA Ops:
  8.6 1.3 %collective-permute-start = (f32[4,2,640]{2,1,0:T(2,128)S(1)}, f32[4,2,640]{2,1,0:T(2,128)S(1)}, u32[]{:S(2)}, u32[]{:S(2)}) collective-permute-start(f32[4,2,640]{2,1,0:T(2,128)S(1)} %get-tuple-element.14.total_ref), channel_id=1, source_target_pairs={{0,4},{4,0},{1,5},{5,1},{2,6},{6,2},{3,7},{7,3},{8,12},{12,8},{9,1... | collective-permute-start | bytes 61448 | tf_op jit(solution)/shard_map/ppermute | solution.py:209
  27.3 1.3 %collective-permute-start.1 = (f32[2,640]{1,0:T(2,128)S(1)}, f32[2,640]{1,0:T(2,128)S(1)}, u32[]{:S(2)}, u32[]{:S(2)}) collective-permute-start(f32[2,640]{1,0:T(2,128)S(1)} %carry.1.mine_ref), channel_id=1, source_target_pairs={{0,4},{4,0},{1,5},{5,1},{2,6},{6,2},{3,7},{7,3},{8,12},{12,8},{9,1... | collective-permute-start | bytes 15368 | tf_op jit(solution)/shard_map/ppermute | solution.py:227
  28.5 11.3 %copy-start = (f32[640]{0:T(1024)S(1)}, f32[640]{0:T(1024)}, u32[]{:S(2)}) copy-start(f32[640]{0:T(1024)} %param.7) | copy-start | bytes 7684
  29.6 5.0 %collective-permute-start.2 = (f32[4,2,1,256]{3,2,1,0:T(1,128)S(1)}, f32[4,2,1,256]{3,2,1,0:T(1,128)S(1)}, u32[]{:S(2)}, u32[]{:S(2)}) collective-permute-start(f32[4,2,1,256]{3,2,1,0:T(1,128)S(1)} %get-tuple-element.16), channel_id=1, source_target_pairs={{0,1},{1,0},{2,3},{3,2},{4,5},{5,4},{6,7},{7,6},{8,9},{9,8},{10,11... | collective-permute-start | bytes 24584 | tf_op jit(solution)/shard_map/ppermute | solution.py:169
  34.6 6.8 %collective-permute-start.3 = (f32[4,2,1,256]{3,2,1,0:T(1,128)S(1)}, f32[4,2,1,256]{3,2,1,0:T(1,128)S(1)}, u32[]{:S(2)}, u32[]{:S(2)}) collective-permute-start(f32[4,2,1,256]{3,2,1,0:T(1,128)S(1)} %add.18), channel_id=1, source_target_pairs={{0,3},{1,2},{2,1},{3,0},{4,7},{5,6},{6,5},{7,4},{8,11},{9,10},{10,... | collective-permute-start | bytes 24584 | tf_op jit(solution)/shard_map/ppermute | solution.py:170

commit v3 on v2

--- a/solution.py
+++ b/solution.py
@@ -9,7 +9,8 @@
 TIME = ("time_0", "time_1", "time_2", "time_3")
 CHIPS = ("time_0", "time_1", "time_2")
 CORE = "time_3"
-CHUNK = 256
+CHUNK = 128
+LOG2E = 1.4426950408889634
 SWAP = [(0, 1), (1, 0)]
 VMEM_LOCAL, VMEM_POWER, VMEM_NORM = 24, 8, 8
 
@@ -34,46 +35,66 @@
             for k, (hbm, ref) in enumerate(pairs)
         ]
 
-    for b in range(batch):
-        for j in range(chunks):
-            for copy in loads(b, j):
-                copy.start()
+    for j in range(chunks):
+        for copy in loads(0, j):
+            copy.start()
 
     row = lax.broadcasted_iota(jnp.int32, (CHUNK, CHUNK), 0)
     col = lax.broadcasted_iota(jnp.int32, (CHUNK, CHUNK), 1)
-    later_ref[...] = jnp.where(col > row, -scale, 0.0).astype(jnp.bfloat16)
-    upto_ref[...] = jnp.where(col > row, 0.0, 1.0).astype(jnp.bfloat16)
-    f32 = jnp.float32
-
-    @pl.loop(0, batch)
+    bf16, f32 = jnp.bfloat16, jnp.float32
+    later_ref[...] = jnp.where(col > row, -scale, 0.0).astype(bf16)
+    upto = jnp.where(col > row, 0.0, 1.0).astype(bf16)
+    upto_ref[:, :CHUNK] = upto
+    upto_ref[:, CHUNK:] = upto
+
+    def chunk(b, j):
+        at = slice(j * CHUNK, (j + 1) * CHUNK)
+        for cols in columns(width):
+            decay = decay_ref[b, at, cols]
+            drive = drive_ref[b, at, cols]
+            logs = jnp.dot(later_ref[...], decay.astype(bf16), preferred_element_type=f32)
+            less = (jnp.exp2(logs * LOG2E) - 1.0).astype(bf16) * drive
+            run = jnp.dot(
+                upto_ref[...], jnp.concatenate([drive, less]), preferred_element_type=f32
+            )
+            run_ref[b, at, cols] = run
+            gate = jnp.tanh((gate_ref[b, at, cols] * bf16(0.5)).astype(f32)) + 1.0
+            open_ref[b, at, cols] = jnp.exp2(logs * -LOG2E) * gate
+            pushed = run[CHUNK - 1 :]
+            lost = jnp.sum(decay, axis=0, keepdims=True) * scale
+            chunk_ref[b, j, 0:1, cols] = lost
+            chunk_ref[b, j, 1:2, cols] = pushed
+            if j == 0:
+                total_ref[b, 0:1, cols] = lost
+                total_ref[b, 1:2, cols] = pushed
+            else:
+                total_ref[b, 0:1, cols] = total_ref[b, 0:1, cols] + lost
+                total_ref[b, 1:2, cols] = jnp.exp(-lost) * total_ref[b, 1:2, cols] + pushed
+
+    for j in range(chunks):
+        for copy in loads(1, j):
+            copy.start()
+    for j in range(chunks):
+        for copy in loads(0, j):
+            copy.wait()
+        for copy in loads(2, j):
+            copy.start()
+        chunk(0, j)
+
+    @pl.loop(1, batch)
     def _(b):
         for j in range(chunks):
             for copy in loads(b, j):
                 copy.wait()
-            at = slice(j * CHUNK, (j + 1) * CHUNK)
-            for cols in columns(width):
-                decay = decay_ref[b, at, cols]
-                drive = drive_ref[b, at, cols]
-                wide = drive.astype(f32)
-                logs = jnp.dot(later_ref[...], decay.astype(jnp.bfloat16), preferred_element_type=f32)
-                weight = jnp.exp(logs)
-                pushed = weight * wide
-                less = (wide - pushed).astype(jnp.bfloat16)
-                run_ref[b, at, cols] = jnp.dot(
-                    upto_ref[...], drive, preferred_element_type=f32
-                ) - jnp.dot(upto_ref[...], less, preferred_element_type=f32)
-                gate = 0.5 * jnp.tanh(0.5 * gate_ref[b, at, cols].astype(f32)) + 0.5
-                open_ref[b, at, cols] = jnp.exp(-logs) * gate
-                pushed = jnp.sum(pushed, axis=0, keepdims=True)
-                lost = jnp.sum(decay, axis=0, keepdims=True) * scale
-                chunk_ref[b, j, 0:1, cols] = lost
-                chunk_ref[b, j, 1:2, cols] = pushed
-                if j == 0:
-                    total_ref[b, 0:1, cols] = lost
-                    total_ref[b, 1:2, cols] = pushed
-                else:
-                    total_ref[b, 0:1, cols] = total_ref[b, 0:1, cols] + lost
-                    total_ref[b, 1:2, cols] = jnp.exp(-lost) * total_ref[b, 1:2, cols] + pushed
+
+        @pl.when(b < batch - 2)
+        def _():
+            for j in range(chunks):
+                for copy in loads(b + 2, j):
+                    copy.start()
+
+        for j in range(chunks):
+            chunk(b, j)
 
 
 def pack_kernel(place_ref, total_ref, other_ref, sent_ref):
@@ -198,7 +219,7 @@
             pltpu.VMEM(shape, jnp.bfloat16),
             pltpu.VMEM(shape, jnp.bfloat16),
             pltpu.VMEM((CHUNK, CHUNK), jnp.bfloat16),
-            pltpu.VMEM((CHUNK, CHUNK), jnp.bfloat16),
+            pltpu.VMEM((CHUNK, 2 * CHUNK), jnp.bfloat16),
             pltpu.SemaphoreType.DMA((3, batch, chunks)),
         ],
         compiler_params=params(VMEM_LOCAL),
@@ -242,7 +263,7 @@
     power = total_over_chan(power)
 
     return pl.pallas_call(
-        lambda *refs: norm_kernel(channels, 1e-6 * total_length, *refs),
+        lambda *refs: norm_kernel(channels, 4e-6 * total_length, *refs),
         in_specs=[vmem] * 3,
         out_specs=hbm,
         out_shape=jax.ShapeDtypeStruct(shape, jnp.bfloat16),

time: 43.6 us -> 41.7 us (0.956)
  Pallas kernels: 11.5 us -> 9.66 us
    pallas_call x1, Pallas kernels: 8.54 us -> 6.58 us  [body(): pl.pallas_call(lambda *refs: local_kernel(1.0 / total_length, *refs), in_...]
where the time goes in v3:
time: 41.7 us; the launch traced here: 41.3 us
  blocking collectives  17.3 us (41%)
  Pallas kernels  9.66 us (23%)
  starting transfers between devices  8.67 us (21%)
  waiting for transfers between devices  5.59 us (13%)
    all_to_all x1, blocking collectives, body(): pieces = lax.all_to_all(sent, CHIPS, 0, 0)  17.3 us
    pallas_call x1, Pallas kernels, body(): pl.pallas_call(lambda *refs: local_kernel(1.0 / total_length, *refs), in_...  6.58 us
    ppermute x1, starting transfers between devices, total_over_chan(): return x + lax.ppermute(x, 'chan', [(i, i ^ 3) for i in range(4)])  5.14 us
    ppermute x1, starting transfers between devices, total_over_chan(): x = x + lax.ppermute(x, 'chan', [(i, i ^ 1) for i in range(4)])  3.35 us
    pallas_call x1, Pallas kernels, body(): pl.pallas_call(lambda *refs: norm_kernel(channels, 4e-06 * total_length,...  1.82 us
    ppermute x1, waiting for transfers between devices, total_over_chan(): x = x + lax.ppermute(x, 'chan', [(i, i ^ 1) for i in range(4)])  1.63 us
    ppermute x1, waiting for transfers between devices, total_over_chan(): return x + lax.ppermute(x, 'chan', [(i, i ^ 3) for i in range(4)])  1.62 us
    ppermute x1, waiting for transfers between devices, body(): other = lax.ppermute(total, CORE, SWAP)  1.18 us
  transfers between devices with their start and end apart: 4, of which 4 were waited for; matrix products, arithmetic and copies ran while one was open for 0% of the time, Pallas kernels for 0%

profile of v3, /device:TPU:2, one launch (start us, length us, event | category | flops | bytes accessed | tf_op | source)
XLA Modules:
  0.0 41.3 jit_solution(13678618599186117645)
XLA Ops:
  0.0 6.6 %local.1 = (f32[4,4,2,640]{3,2,1,0:T(2,128)S(1)}, f32[4,2,640]{2,1,0:T(2,128)S(1)}, f32[4,512,640]{2,1,0:T(8,128)S(1)}, f32[4,512,640]{2,1,0:T(8,128)S(1)}) custom-call(s32[1]{0:T(128)} %bitcast.refs_0_.place_ref, f32[4,512,640]{2,1,0:T(8,128)} %refs_1_.1, bf16[4,512,640]{2,1,0:T(8,128)(2,1)} %refs_2_.1, bf16[4,512,640]{2,1,0:T(8,128)(2,1)} %refs_3_.1), custom_call_target="tpu_custom_call" | custom-call | tf_op jit(solution)/shard_map/local/pallas_call | solution.py:207
  6.6 0.1 collective-permute-start
  6.7 1.2 %collective-permute-done.other_ref = f32[4,2,640]{2,1,0:T(2,128)S(1)} collective-permute-done((f32[4,2,640]{2,1,0:T(2,128)S(1)}, f32[4,2,640]{2,1,0:T(2,128)S(1)}, u32[]{:S(2)}, u32[]{:S(2)}) %collective-permute-start) | collective-permute-done | bytes 20512 | tf_op jit(solution)/shard_map/ppermute | solution.py:230
  7.9 17.3 %all_to_all.5.pieces_ref = f32[32,2,2,640]{3,2,1,0:T(2,128)S(1)} all-to-all(f32[32,2,2,640]{3,2,1,0:T(2,128)S(1)} %pack.1), channel_id=1, replica_groups=mesh['time_0'=2,'time_1'=4,'time_2'=4,'time_3'=2,'chan'=4] {'time_0','ti..., dimensions={0} | all-to-all | bytes 655360 | tf_op jit(solution)/shard_map/all_to_all | solution.py:239
  25.2 0.1 carry.1.mine_ref
  25.3 0.1 collective-permute-start.1
  25.4 1.2 %collective-permute-done.1.across_ref = f32[2,640]{1,0:T(2,128)S(1)} collective-permute-done((f32[2,640]{1,0:T(2,128)S(1)}, f32[2,640]{1,0:T(2,128)S(1)}, u32[]{:S(2)}, u32[]{:S(2)}) %collective-permute-start.1) | collective-permute-done | bytes 5152 | tf_op jit(solution)/shard_map/ppermute | solution.py:248
  26.6 0.0 copy-start
  26.6 1.1 %power.1 = (f32[4,512,640]{2,1,0:T(8,128)S(1)}, f32[4,4,1,128]{3,2,1,0:T(1,128)S(1)}) custom-call(s32[1]{0:T(128)} %bitcast.refs_0_.place_ref, f32[4,512,640]{2,1,0:T(8,128)S(1)} %get-tuple-element.11.run_ref, f32[4,512,640]{2,1,0:T(8,128)S(1)} %get-tuple-element.12.open_ref, f32[4,4,2,640]{3,2,1,0:T(2,128)S(1)} %get-tuple-element.13.chunk_ref, ...), custom_call_target="tpu_custom_call" | custom-call | tf_op jit(solution)/shard_map/power/pallas_call | solution.py:250
  27.7 3.4 %collective-permute-start.2 = (f32[4,4,1,128]{3,2,1,0:T(1,128)S(1)}, f32[4,4,1,128]{3,2,1,0:T(1,128)S(1)}, u32[]{:S(2)}, u32[]{:S(2)}) collective-permute-start(f32[4,4,1,128]{3,2,1,0:T(1,128)S(1)} %get-tuple-element.16), channel_id=1, source_target_pairs={{0,1},{1,0},{2,3},{3,2},{4,5},{5,4},{6,7},{7,6},{8,9},{9,8},{10,11... | collective-permute-start | bytes 24584 | tf_op jit(solution)/shard_map/ppermute | solution.py:190
  31.0 1.6 %collective-permute-done.2 = f32[4,4,1,128]{3,2,1,0:T(1,128)S(1)} collective-permute-done((f32[4,4,1,128]{3,2,1,0:T(1,128)S(1)}, f32[4,4,1,128]{3,2,1,0:T(1,128)S(1)}, u32[]{:S(2)}, u32[]{:S(2)}) %collective-permute-start.2) | collective-permute-done | bytes 8224 | tf_op jit(solution)/shard_map/ppermute | solution.py:190
  32.7 5.1 %collective-permute-start.3 = (f32[4,4,1,128]{3,2,1,0:T(1,128)S(1)}, f32[4,4,1,128]{3,2,1,0:T(1,128)S(1)}, u32[]{:S(2)}, u32[]{:S(2)}) collective-permute-start(f32[4,4,1,128]{3,2,1,0:T(1,128)S(1)} %add.18), channel_id=1, source_target_pairs={{0,3},{1,2},{2,1},{3,0},{4,7},{5,6},{6,5},{7,4},{8,11},{9,10},{10,... | collective-permute-start | bytes 24584 | tf_op jit(solution)/shard_map/ppermute | solution.py:191
  37.8 0.0 copy-done
  37.8 1.6 %collective-permute-done.3 = f32[4,4,1,128]{3,2,1,0:T(1,128)S(1)} collective-permute-done((f32[4,4,1,128]{3,2,1,0:T(1,128)S(1)}, f32[4,4,1,128]{3,2,1,0:T(1,128)S(1)}, u32[]{:S(2)}, u32[]{:S(2)}) %collective-permute-start.3) | collective-permute-done | bytes 8224 | tf_op jit(solution)/shard_map/ppermute | solution.py:191
  39.5 1.8 %norm.1 = bf16[4,512,640]{2,1,0:T(8,128)(2,1)} custom-call(f32[4,512,640]{2,1,0:T(8,128)S(1)} %get-tuple-element.15.refs_0_, f32[4,4,1,128]{3,2,1,0:T(1,128)S(1)} %add.19.refs_1_, f32[1,640]{1,0:T(1,128)S(1)} %broadcast_in_dim.3.refs_2_), custom_call_target="tpu_custom_call" | custom-call | tf_op jit(solution)/shard_map/norm/pallas_call | solution.py:265
  (4 shorter events, 0.1 us)
Async XLA Ops:
  6.6 1.3 %collective-permute-start = (f32[4,2,640]{2,1,0:T(2,128)S(1)}, f32[4,2,640]{2,1,0:T(2,128)S(1)}, u32[]{:S(2)}, u32[]{:S(2)}) collective-permute-start(f32[4,2,640]{2,1,0:T(2,128)S(1)} %get-tuple-element.14.total_ref), channel_id=1, source_target_pairs={{0,4},{4,0},{1,5},{5,1},{2,6},{6,2},{3,7},{7,3},{8,12},{12,8},{9,1... | collective-permute-start | bytes 61448 | tf_op jit(solution)/shard_map/ppermute | solution.py:230
  25.3 1.3 %collective-permute-start.1 = (f32[2,640]{1,0:T(2,128)S(1)}, f32[2,640]{1,0:T(2,128)S(1)}, u32[]{:S(2)}, u32[]{:S(2)}) collective-permute-start(f32[2,640]{1,0:T(2,128)S(1)} %carry.1.mine_ref), channel_id=1, source_target_pairs={{0,4},{4,0},{1,5},{5,1},{2,6},{6,2},{3,7},{7,3},{8,12},{12,8},{9,1... | collective-permute-start | bytes 15368 | tf_op jit(solution)/shard_map/ppermute | solution.py:248
  26.6 11.3 %copy-start = (f32[640]{0:T(1024)S(1)}, f32[640]{0:T(1024)}, u32[]{:S(2)}) copy-start(f32[640]{0:T(1024)} %param.7) | copy-start | bytes 7684
  27.7 5.0 %collective-permute-start.2 = (f32[4,4,1,128]{3,2,1,0:T(1,128)S(1)}, f32[4,4,1,128]{3,2,1,0:T(1,128)S(1)}, u32[]{:S(2)}, u32[]{:S(2)}) collective-permute-start(f32[4,4,1,128]{3,2,1,0:T(1,128)S(1)} %get-tuple-element.16), channel_id=1, source_target_pairs={{0,1},{1,0},{2,3},{3,2},{4,5},{5,4},{6,7},{7,6},{8,9},{9,8},{10,11... | collective-permute-start | bytes 24584 | tf_op jit(solution)/shard_map/ppermute | solution.py:190
  32.7 6.8 %collective-permute-start.3 = (f32[4,4,1,128]{3,2,1,0:T(1,128)S(1)}, f32[4,4,1,128]{3,2,1,0:T(1,128)S(1)}, u32[]{:S(2)}, u32[]{:S(2)}) collective-permute-start(f32[4,4,1,128]{3,2,1,0:T(1,128)S(1)} %add.18), channel_id=1, source_target_pairs={{0,3},{1,2},{2,1},{3,0},{4,7},{5,6},{6,5},{7,4},{8,11},{9,10},{10,... | collective-permute-start | bytes 24584 | tf_op jit(solution)/shard_map/ppermute | solution.py:191

commit v4 on v3

--- a/solution.py
+++ b/solution.py
@@ -20,8 +20,8 @@
 
 
 def local_kernel(
-    scale, place_ref, decay_hbm, drive_hbm, gate_hbm, chunk_ref, total_ref, run_ref, open_ref,
-    decay_ref, drive_ref, gate_ref, later_ref, upto_ref, sems,
+    scale, place_ref, decay_hbm, drive_hbm, gate_hbm, chunk_ref, total_ref, run_ref, logs_ref,
+    gate_ref, decay_ref, drive_ref, later_ref, upto_ref, sems, gate_sem,
 ):
     del place_ref
     batch, length, width = decay_ref.shape
@@ -29,7 +29,7 @@
 
     def loads(b, j):
         at = pl.ds(j * CHUNK, CHUNK)
-        pairs = ((decay_hbm, decay_ref), (drive_hbm, drive_ref), (gate_hbm, gate_ref))
+        pairs = ((decay_hbm, decay_ref), (drive_hbm, drive_ref))
         return [
             pltpu.make_async_copy(hbm.at[b, at], ref.at[b, at], sems.at[k, b, j])
             for k, (hbm, ref) in enumerate(pairs)
@@ -58,8 +58,7 @@
                 upto_ref[...], jnp.concatenate([drive, less]), preferred_element_type=f32
             )
             run_ref[b, at, cols] = run
-            gate = jnp.tanh((gate_ref[b, at, cols] * bf16(0.5)).astype(f32)) + 1.0
-            open_ref[b, at, cols] = jnp.exp2(logs * -LOG2E) * gate
+            logs_ref[b, at, cols] = logs
             pushed = run[CHUNK - 1 :]
             lost = jnp.sum(decay, axis=0, keepdims=True) * scale
             chunk_ref[b, j, 0:1, cols] = lost
@@ -71,6 +70,7 @@
                 total_ref[b, 0:1, cols] = total_ref[b, 0:1, cols] + lost
                 total_ref[b, 1:2, cols] = jnp.exp(-lost) * total_ref[b, 1:2, cols] + pushed
 
+    gates = pltpu.make_async_copy(gate_hbm, gate_ref, gate_sem)
     for j in range(chunks):
         for copy in loads(1, j):
             copy.start()
@@ -93,11 +93,43 @@
                 for copy in loads(b + 2, j):
                     copy.start()
 
+        @pl.when(b == 1)
+        def _():
+            gates.start()
+
         for j in range(chunks):
             chunk(b, j)
 
-
-def pack_kernel(place_ref, total_ref, other_ref, sent_ref):
+    gates.wait()
+
+
+def gate_kernel(gate_ref, twice_ref):
+    batch, length, width = gate_ref.shape
+
+    @pl.loop(0, batch)
+    def _(b):
+        for j in range(length // CHUNK):
+            at = slice(j * CHUNK, (j + 1) * CHUNK)
+            for cols in columns(width):
+                half = (gate_ref[b, at, cols] * jnp.bfloat16(0.5)).astype(jnp.float32)
+                twice_ref[b, at, cols] = jnp.tanh(half) + 1.0
+
+
+def open_kernel(after_ref, logs_ref, twice_ref, open_ref):
+    del after_ref
+    batch, length, width = logs_ref.shape
+
+    @pl.loop(0, batch)
+    def _(b):
+        for j in range(length // CHUNK):
+            at = slice(j * CHUNK, (j + 1) * CHUNK)
+            for cols in columns(width):
+                lift = jnp.exp2(logs_ref[b, at, cols] * -LOG2E)
+                open_ref[b, at, cols] = lift * twice_ref[b, at, cols]
+
+
+def pack_kernel(place_ref, total_ref, other_ref, after_ref, sent_ref):
+    del after_ref
     core = place_ref[0] % 2
     batch = total_ref.shape[0]
 
@@ -204,23 +236,24 @@
     place = lax.axis_index(TIME).astype(jnp.int32).reshape(1)
     smem = pl.BlockSpec(memory_space=pltpu.SMEM)
 
-    chunk, total, run, opened = pl.pallas_call(
+    chunk, total, run, logs, gate = pl.pallas_call(
         lambda *refs: local_kernel(1.0 / total_length, *refs),
         in_specs=[smem, hbm, hbm, hbm],
-        out_specs=[vmem] * 4,
+        out_specs=[vmem] * 5,
         out_shape=[
             jax.ShapeDtypeStruct((batch, chunks, 2, width), f32),
             jax.ShapeDtypeStruct((batch, 2, width), f32),
             jax.ShapeDtypeStruct(shape, f32),
             jax.ShapeDtypeStruct(shape, f32),
+            jax.ShapeDtypeStruct(shape, jnp.bfloat16),
         ],
         scratch_shapes=[
             pltpu.VMEM(shape, f32),
             pltpu.VMEM(shape, jnp.bfloat16),
-            pltpu.VMEM(shape, jnp.bfloat16),
             pltpu.VMEM((CHUNK, CHUNK), jnp.bfloat16),
             pltpu.VMEM((CHUNK, 2 * CHUNK), jnp.bfloat16),
-            pltpu.SemaphoreType.DMA((3, batch, chunks)),
+            pltpu.SemaphoreType.DMA((2, batch, chunks)),
+            pltpu.SemaphoreType.DMA,
         ],
         compiler_params=params(VMEM_LOCAL),
         name="local",
@@ -228,14 +261,24 @@
 
     peers = lax.axis_size(CHIPS)
     other = lax.ppermute(total, CORE, SWAP)
+    small = pl.CostEstimate(flops=1_000_000_000, transcendentals=0, bytes_accessed=0)
+    twice = pl.pallas_call(
+        gate_kernel,
+        in_specs=[vmem],
+        out_specs=vmem,
+        out_shape=jax.ShapeDtypeStruct(shape, f32),
+        compiler_params=params(4),
+        cost_estimate=small,
+        name="gate",
+    )(gate)
     sent = pl.pallas_call(
         pack_kernel,
-        in_specs=[smem, vmem, vmem],
+        in_specs=[smem, vmem, vmem, pl.BlockSpec(memory_space=pl.ANY)],
         out_specs=vmem,
         out_shape=jax.ShapeDtypeStruct((peers, 2, batch // 2, width), f32),
         compiler_params=params(4),
         name="pack",
-    )(place, total, other)
+    )(place, total, other, twice)
     pieces = lax.all_to_all(sent, CHIPS, 0, 0)
     carry = pl.pallas_call(
         carry_kernel,
@@ -246,6 +289,15 @@
         name="carry",
     )(place, pieces)
     across = lax.ppermute(carry, CORE, SWAP)
+    opened = pl.pallas_call(
+        open_kernel,
+        in_specs=[vmem] * 3,
+        out_specs=vmem,
+        out_shape=jax.ShapeDtypeStruct(shape, f32),
+        compiler_params=params(4),
+        cost_estimate=small,
+        name="open",
+    )(carry, logs, twice)
 
     gated, power = pl.pallas_call(
         power_kernel,

time: 41.7 us -> 41.2 us (0.988)
  waiting for transfers between devices: 5.59 us -> 4.13 us
  Pallas kernels: 9.66 us -> 10.6 us
    pallas_call x1 -> x3, Pallas kernels: 0.04 us -> 1.48 us  [the longest x1 0.72 us: body(): pl.pallas_call(gate_kernel, in_specs=[vmem], out_specs=vmem, out_shape=ja...]
    ppermute x1, waiting for transfers between devices: 1.18 us -> 0.45 us  [body(): other = lax.ppermute(total, CORE, SWAP)]
    ppermute x1, waiting for transfers between devices: 1.15 us -> 0.43 us  [body(): across = lax.ppermute(carry, CORE, SWAP)]
    pallas_call x1, Pallas kernels: 6.58 us -> 6.11 us  [body(): pl.pallas_call(lambda *refs: local_kernel(1.0 / total_length, *refs), in_...]
  transfers between devices with their start and end apart: 4 -> 4, of which waited for: 4 -> 4; matrix products, arithmetic and copies ran while one was open for 0% -> 0% of each run, Pallas kernels for 0% -> 4%
where the time goes in v4:
time: 41.2 us; the launch traced here: 40.8 us
  blocking collectives  17.3 us (42%)
  Pallas kernels  10.6 us (26%)
  starting transfers between devices  8.68 us (21%)
  waiting for transfers between devices  4.13 us (10%)
    all_to_all x1, blocking collectives, body(): pieces = lax.all_to_all(sent, CHIPS, 0, 0)  17.3 us
    pallas_call x1, Pallas kernels, body(): pl.pallas_call(lambda *refs: local_kernel(1.0 / total_length, *refs), in_...  6.11 us
    ppermute x1, starting transfers between devices, total_over_chan(): return x + lax.ppermute(x, 'chan', [(i, i ^ 3) for i in range(4)])  5.14 us
    ppermute x1, starting transfers between devices, total_over_chan(): x = x + lax.ppermute(x, 'chan', [(i, i ^ 1) for i in range(4)])  3.36 us
    pallas_call x1, Pallas kernels, body(): pl.pallas_call(lambda *refs: norm_kernel(channels, 4e-06 * total_length,...  1.82 us
    ppermute x1, waiting for transfers between devices, total_over_chan(): x = x + lax.ppermute(x, 'chan', [(i, i ^ 1) for i in range(4)])  1.63 us
    ppermute x1, waiting for transfers between devices, total_over_chan(): return x + lax.ppermute(x, 'chan', [(i, i ^ 3) for i in range(4)])  1.62 us
    pallas_call x1, Pallas kernels, body(): pl.pallas_call(power_kernel, in_specs=[smem] + [vmem] * 6, out_specs=[vme...  1.11 us
  transfers between devices with their start and end apart: 4, of which 4 were waited for; matrix products, arithmetic and copies ran while one was open for 0% of the time, Pallas kernels for 4%

profile of v4, /device:TPU:2, one launch (start us, length us, event | category | flops | bytes accessed | tf_op | source)
XLA Modules:
  0.0 40.8 jit_solution(7335679879938305111)
XLA Ops:
  0.0 6.1 %local.1 = (f32[4,4,2,640]{3,2,1,0:T(2,128)S(1)}, f32[4,2,640]{2,1,0:T(2,128)S(1)}, f32[4,512,640]{2,1,0:T(8,128)S(1)}, f32[4,512,640]{2,1,0:T(8,128)S(1)}, bf16[4,512,640]{2,1,0:T(8,128)(2,1)S(1)}) custom-call(s32[1]{0:T(128)} %bitcast.refs_0_.place_ref, f32[4,512,640]{2,1,0:T(8,128)} %refs_1_.1, bf16[4,512,640]{2,1,0:T(8,128)(2,1)} %refs_2_.1, ...), custom_call_target="tpu_custom_call" | custom-call | tf_op jit(solution)/shard_map/local/pallas_call | solution.py:239
  6.1 0.1 collective-permute-start
  6.2 0.7 %gate.1.after_ref.twice_ref = f32[4,512,640]{2,1,0:T(8,128)S(1)} custom-call(bf16[4,512,640]{2,1,0:T(8,128)(2,1)S(1)} %get-tuple-element.14.gate_ref), custom_call_target="tpu_custom_call" | custom-call | flops 1000000000 | tf_op jit(solution)/shard_map/gate/pallas_call | solution.py:265
  6.9 0.4 %collective-permute-done.other_ref = f32[4,2,640]{2,1,0:T(2,128)S(1)} collective-permute-done((f32[4,2,640]{2,1,0:T(2,128)S(1)}, f32[4,2,640]{2,1,0:T(2,128)S(1)}, u32[]{:S(2)}, u32[]{:S(2)}) %collective-permute-start) | collective-permute-done | bytes 20512 | tf_op jit(solution)/shard_map/ppermute | solution.py:263
  7.4 17.3 %all_to_all.5.pieces_ref = f32[32,2,2,640]{3,2,1,0:T(2,128)S(1)} all-to-all(f32[32,2,2,640]{3,2,1,0:T(2,128)S(1)} %pack.1), channel_id=1, replica_groups=mesh['time_0'=2,'time_1'=4,'time_2'=4,'time_3'=2,'chan'=4] {'time_0','ti..., dimensions={0} | all-to-all | bytes 655360 | tf_op jit(solution)/shard_map/all_to_all | solution.py:282
  24.7 0.1 carry.1.after_ref.mine_ref
  24.8 0.1 collective-permute-start.1
  24.9 0.7 %open.1.open_ref = f32[4,512,640]{2,1,0:T(8,128)S(1)} custom-call(f32[2,640]{1,0:T(2,128)S(1)} %carry.1.after_ref.mine_ref, f32[4,512,640]{2,1,0:T(8,128)S(1)} %get-tuple-element.15.logs_ref, f32[4,512,640]{2,1,0:T(8,128)S(1)} %gate.1.after_ref.twice_ref), custom_call_target="tpu_custom_call" | custom-call | flops 1000000000 | tf_op jit(solution)/shard_map/open/pallas_call | solution.py:292
  25.7 0.4 %collective-permute-done.1.across_ref = f32[2,640]{1,0:T(2,128)S(1)} collective-permute-done((f32[2,640]{1,0:T(2,128)S(1)}, f32[2,640]{1,0:T(2,128)S(1)}, u32[]{:S(2)}, u32[]{:S(2)}) %collective-permute-start.1) | collective-permute-done | bytes 5152 | tf_op jit(solution)/shard_map/ppermute | solution.py:291
  26.1 0.0 copy-start
  26.1 1.1 %power.1 = (f32[4,512,640]{2,1,0:T(8,128)S(1)}, f32[4,4,1,128]{3,2,1,0:T(1,128)S(1)}) custom-call(s32[1]{0:T(128)} %bitcast.refs_0_.place_ref, f32[4,512,640]{2,1,0:T(8,128)S(1)} %get-tuple-element.12.run_ref, f32[4,512,640]{2,1,0:T(8,128)S(1)} %open.1.open_ref, f32[4,4,2,640]{3,2,1,0:T(2,128)S(1)} %get-tuple-element.16.chunk_ref, ...), custom_call_target="tpu_custom_call" | custom-call | tf_op jit(solution)/shard_map/power/pallas_call | solution.py:302
  27.2 3.4 %collective-permute-start.2 = (f32[4,4,1,128]{3,2,1,0:T(1,128)S(1)}, f32[4,4,1,128]{3,2,1,0:T(1,128)S(1)}, u32[]{:S(2)}, u32[]{:S(2)}) collective-permute-start(f32[4,4,1,128]{3,2,1,0:T(1,128)S(1)} %get-tuple-element.18), channel_id=1, source_target_pairs={{0,1},{1,0},{2,3},{3,2},{4,5},{5,4},{6,7},{7,6},{8,9},{9,8},{10,11... | collective-permute-start | bytes 24584 | tf_op jit(solution)/shard_map/ppermute | solution.py:222
  30.6 1.6 %collective-permute-done.2 = f32[4,4,1,128]{3,2,1,0:T(1,128)S(1)} collective-permute-done((f32[4,4,1,128]{3,2,1,0:T(1,128)S(1)}, f32[4,4,1,128]{3,2,1,0:T(1,128)S(1)}, u32[]{:S(2)}, u32[]{:S(2)}) %collective-permute-start.2) | collective-permute-done | bytes 8224 | tf_op jit(solution)/shard_map/ppermute | solution.py:222
  32.2 5.1 %collective-permute-start.3 = (f32[4,4,1,128]{3,2,1,0:T(1,128)S(1)}, f32[4,4,1,128]{3,2,1,0:T(1,128)S(1)}, u32[]{:S(2)}, u32[]{:S(2)}) collective-permute-start(f32[4,4,1,128]{3,2,1,0:T(1,128)S(1)} %add.18), channel_id=1, source_target_pairs={{0,3},{1,2},{2,1},{3,0},{4,7},{5,6},{6,5},{7,4},{8,11},{9,10},{10,... | collective-permute-start | bytes 24584 | tf_op jit(solution)/shard_map/ppermute | solution.py:223
  37.3 0.0 copy-done
  37.3 1.6 %collective-permute-done.3 = f32[4,4,1,128]{3,2,1,0:T(1,128)S(1)} collective-permute-done((f32[4,4,1,128]{3,2,1,0:T(1,128)S(1)}, f32[4,4,1,128]{3,2,1,0:T(1,128)S(1)}, u32[]{:S(2)}, u32[]{:S(2)}) %collective-permute-start.3) | collective-permute-done | bytes 8224 | tf_op jit(solution)/shard_map/ppermute | solution.py:223
  39.0 1.8 %norm.1 = bf16[4,512,640]{2,1,0:T(8,128)(2,1)} custom-call(f32[4,512,640]{2,1,0:T(8,128)S(1)} %get-tuple-element.17.refs_0_, f32[4,4,1,128]{3,2,1,0:T(1,128)S(1)} %add.19.refs_1_, f32[1,640]{1,0:T(1,128)S(1)} %broadcast_in_dim.3.refs_2_), custom_call_target="tpu_custom_call" | custom-call | tf_op jit(solution)/shard_map/norm/pallas_call | solution.py:317
  (4 shorter events, 0.1 us)
Async XLA Ops:
  6.1 1.3 %collective-permute-start = (f32[4,2,640]{2,1,0:T(2,128)S(1)}, f32[4,2,640]{2,1,0:T(2,128)S(1)}, u32[]{:S(2)}, u32[]{:S(2)}) collective-permute-start(f32[4,2,640]{2,1,0:T(2,128)S(1)} %get-tuple-element.13.total_ref), channel_id=1, source_target_pairs={{0,4},{4,0},{1,5},{5,1},{2,6},{6,2},{3,7},{7,3},{8,12},{12,8},{9,1... | collective-permute-start | bytes 61448 | tf_op jit(solution)/shard_map/ppermute | solution.py:263
  24.8 1.3 %collective-permute-start.1 = (f32[2,640]{1,0:T(2,128)S(1)}, f32[2,640]{1,0:T(2,128)S(1)}, u32[]{:S(2)}, u32[]{:S(2)}) collective-permute-start(f32[2,640]{1,0:T(2,128)S(1)} %carry.1.after_ref.mine_ref), channel_id=1, source_target_pairs={{0,4},{4,0},{1,5},{5,1},{2,6},{6,2},{3,7},{7,3},{8,12},{12,8},{9,1... | collective-permute-start | bytes 15368 | tf_op jit(solution)/shard_map/ppermute | solution.py:291
  26.1 11.3 %copy-start = (f32[640]{0:T(1024)S(1)}, f32[640]{0:T(1024)}, u32[]{:S(2)}) copy-start(f32[640]{0:T(1024)} %param.7) | copy-start | bytes 7684
  27.2 5.0 %collective-permute-start.2 = (f32[4,4,1,128]{3,2,1,0:T(1,128)S(1)}, f32[4,4,1,128]{3,2,1,0:T(1,128)S(1)}, u32[]{:S(2)}, u32[]{:S(2)}) collective-permute-start(f32[4,4,1,128]{3,2,1,0:T(1,128)S(1)} %get-tuple-element.18), channel_id=1, source_target_pairs={{0,1},{1,0},{2,3},{3,2},{4,5},{5,4},{6,7},{7,6},{8,9},{9,8},{10,11... | collective-permute-start | bytes 24584 | tf_op jit(solution)/shard_map/ppermute | solution.py:222
  32.2 6.8 %collective-permute-start.3 = (f32[4,4,1,128]{3,2,1,0:T(1,128)S(1)}, f32[4,4,1,128]{3,2,1,0:T(1,128)S(1)}, u32[]{:S(2)}, u32[]{:S(2)}) collective-permute-start(f32[4,4,1,128]{3,2,1,0:T(1,128)S(1)} %add.18), channel_id=1, source_target_pairs={{0,3},{1,2},{2,1},{3,0},{4,7},{5,6},{6,5},{7,4},{8,11},{9,10},{10,... | collective-permute-start | bytes 24584 | tf_op jit(solution)/shard_map/ppermute | solution.py:223

commit v5 on v4

--- a/solution.py
+++ b/solution.py
@@ -161,21 +161,16 @@
     carry_ref[...] = carry
 
 
-def power_kernel(
-    place_ref, run_ref, open_ref, chunk_ref, mine_ref, across_ref, other_ref,
-    gated_ref, power_ref, start_ref,
-):
+def power_kernel(own, place_ref, run_ref, open_ref, chunk_ref, carry_ref, other_ref, *refs):
+    gated_ref, power_ref = refs[-2:]
     batch, length, width = run_ref.shape
     core = place_ref[0] % 2
-    for b in range(batch):
-        h, at = divmod(b, batch // 2)
-        carry = jnp.where(core == h, mine_ref[at : at + 1], across_ref[at : at + 1])
+    begin = (core if own else 1 - core) * (batch // 2)
+    for i in range(batch // 2):
+        b = begin + i
+        carry = carry_ref[i : i + 1]
         passed = jnp.exp(-other_ref[b, 0:1]) * carry + other_ref[b, 1:2]
-        start_ref[b] = jnp.where(core == 0, carry, passed)
-
-    @pl.loop(0, batch)
-    def _(b):
-        carry = start_ref[b]
+        carry = jnp.where(core == 0, carry, passed)
         for j in range(length // CHUNK):
             at = slice(j * CHUNK, (j + 1) * CHUNK)
             kept = carry * jnp.exp(-chunk_ref[b, j, 0:1])
@@ -299,18 +294,21 @@
         name="open",
     )(carry, logs, twice)
 
-    gated, power = pl.pallas_call(
-        power_kernel,
-        in_specs=[smem] + [vmem] * 6,
-        out_specs=[vmem] * 2,
-        out_shape=[
-            jax.ShapeDtypeStruct(shape, f32),
-            jax.ShapeDtypeStruct((batch, chunks, 1, CHUNK), f32),
-        ],
-        scratch_shapes=[pltpu.VMEM((batch, 1, width), f32)],
-        compiler_params=params(VMEM_POWER),
-        name="power",
-    )(place, run, opened, chunk, carry, across, other)
+    def powers(own, carry, *before):
+        return pl.pallas_call(
+            lambda *refs: power_kernel(own, *refs),
+            in_specs=[smem] + [vmem] * (5 + len(before)),
+            out_specs=[vmem] * 2,
+            out_shape=[
+                jax.ShapeDtypeStruct(shape, f32),
+                jax.ShapeDtypeStruct((batch, chunks, 1, CHUNK), f32),
+            ],
+            input_output_aliases={6 + k: k for k in range(len(before))},
+            compiler_params=params(VMEM_POWER),
+            name="own" if own else "rest",
+        )(place, run, opened, chunk, carry, other, *before)
+
+    gated, power = powers(False, across, *powers(True, carry))
 
     power = total_over_chan(power)
 

time: 41.2 us -> 41 us (level)
  waiting for transfers between devices: 4.13 us -> 3.71 us
    ppermute x1, waiting for transfers between devices: 0.43 us -> 0.01 us  [body(): across = lax.ppermute(carry, CORE, SWAP)]
    pallas_call x1 -> x2, Pallas kernels: 1.11 us -> 0.96 us  [powers(): pl.pallas_call(lambda *refs: power_kernel(own, *refs), in_specs=[smem] +...]
  transfers between devices with their start and end apart: 4 -> 4, of which waited for: 4 -> 3; matrix products, arithmetic and copies ran while one was open for 0% -> 0% of each run, Pallas kernels for 4% -> 5%
where the time goes in v5:
time: 41 us; the launch traced here: 40.2 us
  blocking collectives  17.3 us (42%)
  Pallas kernels  10.5 us (26%)
  starting transfers between devices  8.68 us (21%)
  waiting for transfers between devices  3.71 us (9%)
    all_to_all x1, blocking collectives, body(): pieces = lax.all_to_all(sent, CHIPS, 0, 0)  17.3 us
    pallas_call x1, Pallas kernels, body(): pl.pallas_call(lambda *refs: local_kernel(1.0 / total_length, *refs), in_...  6.11 us
    ppermute x1, starting transfers between devices, total_over_chan(): return x + lax.ppermute(x, 'chan', [(i, i ^ 3) for i in range(4)])  5.14 us
    ppermute x1, starting transfers between devices, total_over_chan(): x = x + lax.ppermute(x, 'chan', [(i, i ^ 1) for i in range(4)])  3.36 us
    pallas_call x1, Pallas kernels, body(): pl.pallas_call(lambda *refs: norm_kernel(channels, 4e-06 * total_length,...  1.82 us
    ppermute x1, waiting for transfers between devices, total_over_chan(): x = x + lax.ppermute(x, 'chan', [(i, i ^ 1) for i in range(4)])  1.63 us
    ppermute x1, waiting for transfers between devices, total_over_chan(): return x + lax.ppermute(x, 'chan', [(i, i ^ 3) for i in range(4)])  1.62 us
    pallas_call x2, Pallas kernels, powers(): pl.pallas_call(lambda *refs: power_kernel(own, *refs), in_specs=[smem] +...  0.96 us
  transfers between devices with their start and end apart: 4, of which 3 were waited for; matrix products, arithmetic and copies ran while one was open for 0% of the time, Pallas kernels for 5%

profile of v5, /device:TPU:2, one launch (start us, length us, event | category | flops | bytes accessed | tf_op | source)
XLA Modules:
  0.0 40.2 jit_solution(14358996394604528346)
XLA Ops:
  0.0 6.1 %local.1 = (f32[4,4,2,640]{3,2,1,0:T(2,128)S(1)}, f32[4,2,640]{2,1,0:T(2,128)S(1)}, f32[4,512,640]{2,1,0:T(8,128)S(1)}, f32[4,512,640]{2,1,0:T(8,128)S(1)}, bf16[4,512,640]{2,1,0:T(8,128)(2,1)S(1)}) custom-call(s32[1]{0:T(128)} %bitcast.refs_0_.place_ref, f32[4,512,640]{2,1,0:T(8,128)} %refs_1_.1, bf16[4,512,640]{2,1,0:T(8,128)(2,1)} %refs_2_.1, ...), custom_call_target="tpu_custom_call" | custom-call | tf_op jit(solution)/shard_map/local/pallas_call | solution.py:234
  6.1 0.1 collective-permute-start
  6.2 0.7 %gate.1.after_ref.twice_ref = f32[4,512,640]{2,1,0:T(8,128)S(1)} custom-call(bf16[4,512,640]{2,1,0:T(8,128)(2,1)S(1)} %get-tuple-element.16.gate_ref), custom_call_target="tpu_custom_call" | custom-call | flops 1000000000 | tf_op jit(solution)/shard_map/gate/pallas_call | solution.py:260
  6.9 0.4 %collective-permute-done.other_ref.refs_5_ = f32[4,2,640]{2,1,0:T(2,128)S(1)} collective-permute-done((f32[4,2,640]{2,1,0:T(2,128)S(1)}, f32[4,2,640]{2,1,0:T(2,128)S(1)}, u32[]{:S(2)}, u32[]{:S(2)}) %collective-permute-start) | collective-permute-done | bytes 20512 | tf_op jit(solution)/shard_map/ppermute | solution.py:258
  7.4 17.3 %all_to_all.5.pieces_ref = f32[32,2,2,640]{3,2,1,0:T(2,128)S(1)} all-to-all(f32[32,2,2,640]{3,2,1,0:T(2,128)S(1)} %pack.1), channel_id=1, replica_groups=mesh['time_0'=2,'time_1'=4,'time_2'=4,'time_3'=2,'chan'=4] {'time_0','ti..., dimensions={0} | all-to-all | bytes 655360 | tf_op jit(solution)/shard_map/all_to_all | solution.py:277
  24.7 0.1 carry.1.after_ref.refs_4_
  24.8 0.1 collective-permute-start.1
  24.9 0.7 %open.1.refs_2_ = f32[4,512,640]{2,1,0:T(8,128)S(1)} custom-call(f32[2,640]{1,0:T(2,128)S(1)} %carry.1.after_ref.refs_4_, f32[4,512,640]{2,1,0:T(8,128)S(1)} %get-tuple-element.17.logs_ref, f32[4,512,640]{2,1,0:T(8,128)S(1)} %gate.1.after_ref.twice_ref), custom_call_target="tpu_custom_call" | custom-call | flops 1000000000 | tf_op jit(solution)/shard_map/open/pallas_call | solution.py:287
  25.7 0.5 %own.1 = (f32[4,512,640]{2,1,0:T(8,128)S(1)}, f32[4,4,1,128]{3,2,1,0:T(1,128)S(1)}) custom-call(s32[1]{0:T(128)} %bitcast.refs_0_.place_ref, f32[4,512,640]{2,1,0:T(8,128)S(1)} %get-tuple-element.14.refs_1_, f32[4,512,640]{2,1,0:T(8,128)S(1)} %open.1.refs_2_, f32[4,4,2,640]{3,2,1,0:T(2,128)S(1)} %get-tuple-element.18.refs_3_, ...), custom_call_target="tpu_custom_call" | custom-call | tf_op jit(solution)/shard_map/own/pallas_call | solution.py:298
  26.1 0.0 collective-permute-done.1.refs_4_
  26.1 0.0 copy-start
  26.2 0.5 %rest.1 = (f32[4,512,640]{2,1,0:T(8,128)S(1)}, f32[4,4,1,128]{3,2,1,0:T(1,128)S(1)}) custom-call(s32[1]{0:T(128)} %bitcast.refs_0_.place_ref, f32[4,512,640]{2,1,0:T(8,128)S(1)} %get-tuple-element.14.refs_1_, f32[4,512,640]{2,1,0:T(8,128)S(1)} %open.1.refs_2_, ...), custom_call_target="tpu_custom_call", output_to_operand_aliasing={{0}: (6, {}), {1}: (7, {})} | custom-call | tf_op jit(solution)/shard_map/rest/pallas_call | solution.py:298
  26.6 3.4 %collective-permute-start.2 = (f32[4,4,1,128]{3,2,1,0:T(1,128)S(1)}, f32[4,4,1,128]{3,2,1,0:T(1,128)S(1)}, u32[]{:S(2)}, u32[]{:S(2)}) collective-permute-start(f32[4,4,1,128]{3,2,1,0:T(1,128)S(1)} %get-tuple-element.22), channel_id=1, source_target_pairs={{0,1},{1,0},{2,3},{3,2},{4,5},{5,4},{6,7},{7,6},{8,9},{9,8},{10,11... | collective-permute-start | bytes 24584 | tf_op jit(solution)/shard_map/ppermute | solution.py:217
  30.0 1.6 %collective-permute-done.2 = f32[4,4,1,128]{3,2,1,0:T(1,128)S(1)} collective-permute-done((f32[4,4,1,128]{3,2,1,0:T(1,128)S(1)}, f32[4,4,1,128]{3,2,1,0:T(1,128)S(1)}, u32[]{:S(2)}, u32[]{:S(2)}) %collective-permute-start.2) | collective-permute-done | bytes 8224 | tf_op jit(solution)/shard_map/ppermute | solution.py:217
  31.6 5.1 %collective-permute-start.3 = (f32[4,4,1,128]{3,2,1,0:T(1,128)S(1)}, f32[4,4,1,128]{3,2,1,0:T(1,128)S(1)}, u32[]{:S(2)}, u32[]{:S(2)}) collective-permute-start(f32[4,4,1,128]{3,2,1,0:T(1,128)S(1)} %add.18), channel_id=1, source_target_pairs={{0,3},{1,2},{2,1},{3,0},{4,7},{5,6},{6,5},{7,4},{8,11},{9,10},{10,... | collective-permute-start | bytes 24584 | tf_op jit(solution)/shard_map/ppermute | solution.py:218
  36.8 0.0 copy-done
  36.8 1.6 %collective-permute-done.3 = f32[4,4,1,128]{3,2,1,0:T(1,128)S(1)} collective-permute-done((f32[4,4,1,128]{3,2,1,0:T(1,128)S(1)}, f32[4,4,1,128]{3,2,1,0:T(1,128)S(1)}, u32[]{:S(2)}, u32[]{:S(2)}) %collective-permute-start.3) | collective-permute-done | bytes 8224 | tf_op jit(solution)/shard_map/ppermute | solution.py:218
  38.4 1.8 %norm.1 = bf16[4,512,640]{2,1,0:T(8,128)(2,1)} custom-call(f32[4,512,640]{2,1,0:T(8,128)S(1)} %get-tuple-element.21.refs_0_, f32[4,4,1,128]{3,2,1,0:T(1,128)S(1)} %add.19.refs_1_, f32[1,640]{1,0:T(1,128)S(1)} %broadcast_in_dim.3.refs_2_), custom_call_target="tpu_custom_call" | custom-call | tf_op jit(solution)/shard_map/norm/pallas_call | solution.py:315
  (4 shorter events, 0.1 us)
Async XLA Ops:
  6.1 1.3 %collective-permute-start = (f32[4,2,640]{2,1,0:T(2,128)S(1)}, f32[4,2,640]{2,1,0:T(2,128)S(1)}, u32[]{:S(2)}, u32[]{:S(2)}) collective-permute-start(f32[4,2,640]{2,1,0:T(2,128)S(1)} %get-tuple-element.15.total_ref), channel_id=1, source_target_pairs={{0,4},{4,0},{1,5},{5,1},{2,6},{6,2},{3,7},{7,3},{8,12},{12,8},{9,1... | collective-permute-start | bytes 61448 | tf_op jit(solution)/shard_map/ppermute | solution.py:258
  24.8 1.3 %collective-permute-start.1 = (f32[2,640]{1,0:T(2,128)S(1)}, f32[2,640]{1,0:T(2,128)S(1)}, u32[]{:S(2)}, u32[]{:S(2)}) collective-permute-start(f32[2,640]{1,0:T(2,128)S(1)} %carry.1.after_ref.refs_4_), channel_id=1, source_target_pairs={{0,4},{4,0},{1,5},{5,1},{2,6},{6,2},{3,7},{7,3},{8,12},{12,8},{9,1... | collective-permute-start | bytes 15368 | tf_op jit(solution)/shard_map/ppermute | solution.py:286
  26.1 10.6 %copy-start = (f32[640]{0:T(1024)S(1)}, f32[640]{0:T(1024)}, u32[]{:S(2)}) copy-start(f32[640]{0:T(1024)} %param.7) | copy-start | bytes 7684
  26.6 5.0 %collective-permute-start.2 = (f32[4,4,1,128]{3,2,1,0:T(1,128)S(1)}, f32[4,4,1,128]{3,2,1,0:T(1,128)S(1)}, u32[]{:S(2)}, u32[]{:S(2)}) collective-permute-start(f32[4,4,1,128]{3,2,1,0:T(1,128)S(1)} %get-tuple-element.22), channel_id=1, source_target_pairs={{0,1},{1,0},{2,3},{3,2},{4,5},{5,4},{6,7},{7,6},{8,9},{9,8},{10,11... | collective-permute-start | bytes 24584 | tf_op jit(solution)/shard_map/ppermute | solution.py:217
  31.6 6.8 %collective-permute-start.3 = (f32[4,4,1,128]{3,2,1,0:T(1,128)S(1)}, f32[4,4,1,128]{3,2,1,0:T(1,128)S(1)}, u32[]{:S(2)}, u32[]{:S(2)}) collective-permute-start(f32[4,4,1,128]{3,2,1,0:T(1,128)S(1)} %add.18), channel_id=1, source_target_pairs={{0,3},{1,2},{2,1},{3,0},{4,7},{5,6},{6,5},{7,4},{8,11},{9,10},{10,... | collective-permute-start | bytes 24584 | tf_op jit(solution)/shard_map/ppermute | solution.py:218

commit v6 on v5

--- a/solution.py
+++ b/solution.py
@@ -71,32 +71,29 @@
                 total_ref[b, 1:2, cols] = jnp.exp(-lost) * total_ref[b, 1:2, cols] + pushed
 
     gates = pltpu.make_async_copy(gate_hbm, gate_ref, gate_sem)
-    for j in range(chunks):
-        for copy in loads(1, j):
+    def whole(b):
+        pairs = ((decay_hbm, decay_ref), (drive_hbm, drive_ref))
+        return [
+            pltpu.make_async_copy(hbm.at[b], ref.at[b], sems.at[k, b, 0])
+            for k, (hbm, ref) in enumerate(pairs)
+        ]
+
+    for b in (1, 2):
+        for copy in whole(b):
             copy.start()
     for j in range(chunks):
         for copy in loads(0, j):
             copy.wait()
-        for copy in loads(2, j):
-            copy.start()
+        if j == 0:
+            for copy in whole(3):
+                copy.start()
+            gates.start()
         chunk(0, j)
 
     @pl.loop(1, batch)
     def _(b):
-        for j in range(chunks):
-            for copy in loads(b, j):
-                copy.wait()
-
-        @pl.when(b < batch - 2)
-        def _():
-            for j in range(chunks):
-                for copy in loads(b + 2, j):
-                    copy.start()
-
-        @pl.when(b == 1)
-        def _():
-            gates.start()
-
+        for copy in whole(b):
+            copy.wait()
         for j in range(chunks):
             chunk(b, j)
 

time: 41 us -> 41 us (level)
  no operation moved by 1% of the time
where the time goes in v6:
time: 41 us; the launch traced here: 40.2 us
  blocking collectives  17.3 us (42%)
  Pallas kernels  10.4 us (25%)
  starting transfers between devices  8.68 us (21%)
  waiting for transfers between devices  3.71 us (9%)
    all_to_all x1, blocking collectives, body(): pieces = lax.all_to_all(sent, CHIPS, 0, 0)  17.3 us
    pallas_call x1, Pallas kernels, body(): pl.pallas_call(lambda *refs: local_kernel(1.0 / total_length, *refs), in_...  6.07 us
    ppermute x1, starting transfers between devices, total_over_chan(): return x + lax.ppermute(x, 'chan', [(i, i ^ 3) for i in range(4)])  5.14 us
    ppermute x1, starting transfers between devices, total_over_chan(): x = x + lax.ppermute(x, 'chan', [(i, i ^ 1) for i in range(4)])  3.36 us
    pallas_call x1, Pallas kernels, body(): pl.pallas_call(lambda *refs: norm_kernel(channels, 4e-06 * total_length,...  1.82 us
    ppermute x1, waiting for transfers between devices, total_over_chan(): x = x + lax.ppermute(x, 'chan', [(i, i ^ 1) for i in range(4)])  1.63 us
    ppermute x1, waiting for transfers between devices, total_over_chan(): return x + lax.ppermute(x, 'chan', [(i, i ^ 3) for i in range(4)])  1.62 us
    pallas_call x2, Pallas kernels, powers(): pl.pallas_call(lambda *refs: power_kernel(own, *refs), in_specs=[smem] +...  0.96 us
  transfers between devices with their start and end apart: 4, of which 3 were waited for; matrix products, arithmetic and copies ran while one was open for 0% of the time, Pallas kernels for 5%

profile of v6, /device:TPU:2, one launch (start us, length us, event | category | flops | bytes accessed | tf_op | source)
XLA Modules:
  0.0 40.2 jit_solution(17464684701226076853)
XLA Ops:
  0.0 6.1 %local.1 = (f32[4,4,2,640]{3,2,1,0:T(2,128)S(1)}, f32[4,2,640]{2,1,0:T(2,128)S(1)}, f32[4,512,640]{2,1,0:T(8,128)S(1)}, f32[4,512,640]{2,1,0:T(8,128)S(1)}, bf16[4,512,640]{2,1,0:T(8,128)(2,1)S(1)}) custom-call(s32[1]{0:T(128)} %bitcast.refs_0_.place_ref, f32[4,512,640]{2,1,0:T(8,128)} %refs_1_.1, bf16[4,512,640]{2,1,0:T(8,128)(2,1)} %refs_2_.1, ...), custom_call_target="tpu_custom_call" | custom-call | tf_op jit(solution)/shard_map/local/pallas_call | solution.py:231
  6.1 0.1 collective-permute-start
  6.2 0.7 %gate.1.after_ref.twice_ref = f32[4,512,640]{2,1,0:T(8,128)S(1)} custom-call(bf16[4,512,640]{2,1,0:T(8,128)(2,1)S(1)} %get-tuple-element.16.gate_ref), custom_call_target="tpu_custom_call" | custom-call | flops 1000000000 | tf_op jit(solution)/shard_map/gate/pallas_call | solution.py:257
  6.9 0.4 %collective-permute-done.other_ref.refs_5_ = f32[4,2,640]{2,1,0:T(2,128)S(1)} collective-permute-done((f32[4,2,640]{2,1,0:T(2,128)S(1)}, f32[4,2,640]{2,1,0:T(2,128)S(1)}, u32[]{:S(2)}, u32[]{:S(2)}) %collective-permute-start) | collective-permute-done | bytes 20512 | tf_op jit(solution)/shard_map/ppermute | solution.py:255
  7.4 17.3 %all_to_all.5.pieces_ref = f32[32,2,2,640]{3,2,1,0:T(2,128)S(1)} all-to-all(f32[32,2,2,640]{3,2,1,0:T(2,128)S(1)} %pack.1), channel_id=1, replica_groups=mesh['time_0'=2,'time_1'=4,'time_2'=4,'time_3'=2,'chan'=4] {'time_0','ti..., dimensions={0} | all-to-all | bytes 655360 | tf_op jit(solution)/shard_map/all_to_all | solution.py:274
  24.7 0.1 carry.1.after_ref.refs_4_
  24.8 0.1 collective-permute-start.1
  24.9 0.7 %open.1.refs_2_ = f32[4,512,640]{2,1,0:T(8,128)S(1)} custom-call(f32[2,640]{1,0:T(2,128)S(1)} %carry.1.after_ref.refs_4_, f32[4,512,640]{2,1,0:T(8,128)S(1)} %get-tuple-element.17.logs_ref, f32[4,512,640]{2,1,0:T(8,128)S(1)} %gate.1.after_ref.twice_ref), custom_call_target="tpu_custom_call" | custom-call | flops 1000000000 | tf_op jit(solution)/shard_map/open/pallas_call | solution.py:284
  25.6 0.5 %own.1 = (f32[4,512,640]{2,1,0:T(8,128)S(1)}, f32[4,4,1,128]{3,2,1,0:T(1,128)S(1)}) custom-call(s32[1]{0:T(128)} %bitcast.refs_0_.place_ref, f32[4,512,640]{2,1,0:T(8,128)S(1)} %get-tuple-element.14.refs_1_, f32[4,512,640]{2,1,0:T(8,128)S(1)} %open.1.refs_2_, f32[4,4,2,640]{3,2,1,0:T(2,128)S(1)} %get-tuple-element.18.refs_3_, ...), custom_call_target="tpu_custom_call" | custom-call | tf_op jit(solution)/shard_map/own/pallas_call | solution.py:295
  26.1 0.0 collective-permute-done.1.refs_4_
  26.1 0.0 copy-start
  26.1 0.5 %rest.1 = (f32[4,512,640]{2,1,0:T(8,128)S(1)}, f32[4,4,1,128]{3,2,1,0:T(1,128)S(1)}) custom-call(s32[1]{0:T(128)} %bitcast.refs_0_.place_ref, f32[4,512,640]{2,1,0:T(8,128)S(1)} %get-tuple-element.14.refs_1_, f32[4,512,640]{2,1,0:T(8,128)S(1)} %open.1.refs_2_, ...), custom_call_target="tpu_custom_call", output_to_operand_aliasing={{0}: (6, {}), {1}: (7, {})} | custom-call | tf_op jit(solution)/shard_map/rest/pallas_call | solution.py:295
  26.6 3.4 %collective-permute-start.2 = (f32[4,4,1,128]{3,2,1,0:T(1,128)S(1)}, f32[4,4,1,128]{3,2,1,0:T(1,128)S(1)}, u32[]{:S(2)}, u32[]{:S(2)}) collective-permute-start(f32[4,4,1,128]{3,2,1,0:T(1,128)S(1)} %get-tuple-element.22), channel_id=1, source_target_pairs={{0,1},{1,0},{2,3},{3,2},{4,5},{5,4},{6,7},{7,6},{8,9},{9,8},{10,11... | collective-permute-start | bytes 24584 | tf_op jit(solution)/shard_map/ppermute | solution.py:214
  30.0 1.6 %collective-permute-done.2 = f32[4,4,1,128]{3,2,1,0:T(1,128)S(1)} collective-permute-done((f32[4,4,1,128]{3,2,1,0:T(1,128)S(1)}, f32[4,4,1,128]{3,2,1,0:T(1,128)S(1)}, u32[]{:S(2)}, u32[]{:S(2)}) %collective-permute-start.2) | collective-permute-done | bytes 8224 | tf_op jit(solution)/shard_map/ppermute | solution.py:214
  31.6 5.1 %collective-permute-start.3 = (f32[4,4,1,128]{3,2,1,0:T(1,128)S(1)}, f32[4,4,1,128]{3,2,1,0:T(1,128)S(1)}, u32[]{:S(2)}, u32[]{:S(2)}) collective-permute-start(f32[4,4,1,128]{3,2,1,0:T(1,128)S(1)} %add.18), channel_id=1, source_target_pairs={{0,3},{1,2},{2,1},{3,0},{4,7},{5,6},{6,5},{7,4},{8,11},{9,10},{10,... | collective-permute-start | bytes 24584 | tf_op jit(solution)/shard_map/ppermute | solution.py:215
  36.7 0.0 copy-done
  36.7 1.6 %collective-permute-done.3 = f32[4,4,1,128]{3,2,1,0:T(1,128)S(1)} collective-permute-done((f32[4,4,1,128]{3,2,1,0:T(1,128)S(1)}, f32[4,4,1,128]{3,2,1,0:T(1,128)S(1)}, u32[]{:S(2)}, u32[]{:S(2)}) %collective-permute-start.3) | collective-permute-done | bytes 8224 | tf_op jit(solution)/shard_map/ppermute | solution.py:215
  38.4 1.8 %norm.1 = bf16[4,512,640]{2,1,0:T(8,128)(2,1)} custom-call(f32[4,512,640]{2,1,0:T(8,128)S(1)} %get-tuple-element.21.refs_0_, f32[4,4,1,128]{3,2,1,0:T(1,128)S(1)} %add.19.refs_1_, f32[1,640]{1,0:T(1,128)S(1)} %broadcast_in_dim.3.refs_2_), custom_call_target="tpu_custom_call" | custom-call | tf_op jit(solution)/shard_map/norm/pallas_call | solution.py:312
  (4 shorter events, 0.1 us)
Async XLA Ops:
  6.1 1.3 %collective-permute-start = (f32[4,2,640]{2,1,0:T(2,128)S(1)}, f32[4,2,640]{2,1,0:T(2,128)S(1)}, u32[]{:S(2)}, u32[]{:S(2)}) collective-permute-start(f32[4,2,640]{2,1,0:T(2,128)S(1)} %get-tuple-element.15.total_ref), channel_id=1, source_target_pairs={{0,4},{4,0},{1,5},{5,1},{2,6},{6,2},{3,7},{7,3},{8,12},{12,8},{9,1... | collective-permute-start | bytes 61448 | tf_op jit(solution)/shard_map/ppermute | solution.py:255
  24.8 1.3 %collective-permute-start.1 = (f32[2,640]{1,0:T(2,128)S(1)}, f32[2,640]{1,0:T(2,128)S(1)}, u32[]{:S(2)}, u32[]{:S(2)}) collective-permute-start(f32[2,640]{1,0:T(2,128)S(1)} %carry.1.after_ref.refs_4_), channel_id=1, source_target_pairs={{0,4},{4,0},{1,5},{5,1},{2,6},{6,2},{3,7},{7,3},{8,12},{12,8},{9,1... | collective-permute-start | bytes 15368 | tf_op jit(solution)/shard_map/ppermute | solution.py:283
  26.1 10.6 %copy-start = (f32[640]{0:T(1024)S(1)}, f32[640]{0:T(1024)}, u32[]{:S(2)}) copy-start(f32[640]{0:T(1024)} %param.7) | copy-start | bytes 7684
  26.6 5.0 %collective-permute-start.2 = (f32[4,4,1,128]{3,2,1,0:T(1,128)S(1)}, f32[4,4,1,128]{3,2,1,0:T(1,128)S(1)}, u32[]{:S(2)}, u32[]{:S(2)}) collective-permute-start(f32[4,4,1,128]{3,2,1,0:T(1,128)S(1)} %get-tuple-element.22), channel_id=1, source_target_pairs={{0,1},{1,0},{2,3},{3,2},{4,5},{5,4},{6,7},{7,6},{8,9},{9,8},{10,11... | collective-permute-start | bytes 24584 | tf_op jit(solution)/shard_map/ppermute | solution.py:214
  31.6 6.8 %collective-permute-start.3 = (f32[4,4,1,128]{3,2,1,0:T(1,128)S(1)}, f32[4,4,1,128]{3,2,1,0:T(1,128)S(1)}, u32[]{:S(2)}, u32[]{:S(2)}) collective-permute-start(f32[4,4,1,128]{3,2,1,0:T(1,128)S(1)} %add.18), channel_id=1, source_target_pairs={{0,3},{1,2},{2,1},{3,0},{4,7},{5,6},{6,5},{7,4},{8,11},{9,10},{10,... | collective-permute-start | bytes 24584 | tf_op jit(solution)/shard_map/ppermute | solution.py:215
